TPU v7x, 256 devices: a whole 4x4x8 slice. The times are simulated.
256 devices in a mesh: row: 32 (over x, y, core), col: 8 (over z).
Axes of the slice: x: 4, y: 4, z: 8, core: 2. Of those that a mesh axis runs over, the one named last changes fastest.
Arguments:
- state: float32 [9, 35, 65536], P(None, None, ('col', 'row')), may hold values from -6 to 6
- geometry: bfloat16 [9, 128, 65536], P(None, 'row', 'col'), may hold values from -5 to 5
- material: float32 [4, 65536], P(None, ('col', 'row')), may hold values from 0.5 to 2
- neighbours: int32 [4, 4, 65536], P(None, None, ('col', 'row')), may hold values from 0 to 1023, as said below
- send_faces: int32 [256, 8, 64], P(('col', 'row')), may hold values from 0 to 1023, as said below
- vol_eval: float32 [35, 128], replicated, may hold values from -1 to 1
- vol_grad: bfloat16 [3, 35, 128], replicated, may hold values from -0.3125 to 0.3125
- face_eval: float32 [4, 35, 27], replicated, may hold values from -1 to 1
- face_lift: float32 [4, 35, 27], replicated, may hold values from -0.625 to 0.625
- normals: bfloat16 [3, 27, 4, 65536], P(None, None, None, ('col', 'row')), may hold values from -5 to 5
- areas: float32 [27, 4, 65536], P(None, None, ('col', 'row')), may hold values from 0.5 to 2
Outputs:
- section: float32 [9, 35, 65536], P(None, None, ('col', 'row'))
Inputs may be any that keep to these rules, and one draw needn't show every extreme that they name: `neighbours`: field 0 is the kind: 0 the neighbour face lies in the same block, 1 in another block of the same row group, 2 free surface, 3 absorbing. Field 1 is the neighbour block's col index (the own col index for kinds 0, 2, 3). Field 2 is, for kind 0, the neighbour's face number f * 256 + e within the block; for kind 1, a slot below the number of faces that the neighbour's block lists for this block in send_faces; else 0. Field 3 is an orientation of 0 to 2 (0 for kinds 2 and 3). Neighbouring is mutual: the neighbour face names this face back, with orientation (3 - turn) % 3. `send_faces`: A block lists at most 64 faces for one col index, the same number as that block lists back, and nothing for its own col index; entries past the count are 0. In every row group some pair of blocks lists exactly 64 faces to each other.
All inputs are finite; a program needn't handle non-finite values.
Results may differ from a plain program's by a relative error of at most 0.0065.
Values may be sent and summed in bfloat16 or wider, within the bound.
A program may use at most 64 MiB of HBM per device.

v0:
```python
import jax
import jax.numpy as jnp
from jax import lax
from jax.sharding import Mesh
from jax.sharding import PartitionSpec as P

ROW = ("row_0", "row_1", "row_2")
COL_ROW = ("col", "row_0", "row_1", "row_2")


HIGHEST = lax.Precision.HIGHEST


def split_up(value, dim, length):
    lengths = value.shape
    blocks = value.reshape(*lengths[:dim], length, lengths[dim] // length, *lengths[dim + 1 :])
    return jnp.moveaxis(blocks, dim, 0)


def in_order(blocks, dim):
    blocks = jnp.moveaxis(blocks, 0, dim)
    lengths = blocks.shape
    return blocks.reshape(*lengths[:dim], lengths[dim] * lengths[dim + 1], *lengths[dim + 2 :])


def turned_blocks(blocks, axes, turns):
    inside = blocks.shape[1:]
    result = blocks.reshape(*(lax.axis_size(a) for a in axes), *inside)
    for k in turns:
        result = lax.all_to_all(result, axes[k], k, k, tiled=True)
    return result.reshape(-1, *inside)


def core_and_chips(value, groups, turns, split_dim, concat_dim):
    length = lax.axis_size(groups[0]) * lax.axis_size(groups[1])
    blocks = split_up(value, split_dim, length)
    return in_order(turned_blocks(blocks, groups, turns), concat_dim)


def normal_flux(values, lame_first, rigidity, buoyancy, normal):
    velocity = values[6:9]
    stress = values[0:6]
    normal_speed = velocity[0] * normal[0] + velocity[1] * normal[1] + velocity[2] * normal[2]
    pressure = lame_first * normal_speed
    components = [
        -(pressure + 2.0 * rigidity * normal[0] * velocity[0]),
        -(pressure + 2.0 * rigidity * normal[1] * velocity[1]),
        -(pressure + 2.0 * rigidity * normal[2] * velocity[2]),
        -rigidity * (normal[0] * velocity[1] + normal[1] * velocity[0]),
        -rigidity * (normal[1] * velocity[2] + normal[2] * velocity[1]),
        -rigidity * (normal[0] * velocity[2] + normal[2] * velocity[0]),
        -buoyancy * (stress[0] * normal[0] + stress[3] * normal[1] + stress[5] * normal[2]),
        -buoyancy * (stress[3] * normal[0] + stress[1] * normal[1] + stress[4] * normal[2]),
        -buoyancy * (stress[5] * normal[0] + stress[4] * normal[1] + stress[2] * normal[2]),
    ]
    return jnp.stack(components)


def volume_fluxes(points, metric, material):
    values = points.astype(jnp.float32)
    result = []
    for direction in range(3):
        normal = (metric[3 * direction], metric[3 * direction + 1], metric[3 * direction + 2])
        result.append(normal_flux(values, material[0], material[1], material[2], normal))
    return jnp.stack(result).astype(jnp.bfloat16)


def rotate_points(gathered, turning):
    full_shape = gathered.shape
    grouped = gathered.reshape(full_shape[0], full_shape[1] // 3, 3, full_shape[2], full_shape[3])
    rotated_one = jnp.roll(grouped, -1, axis=2).reshape(full_shape)
    rotated_two = jnp.roll(grouped, -2, axis=2).reshape(full_shape)
    return jnp.where(turning == 0, gathered, jnp.where(turning == 1, rotated_one, rotated_two))


def exterior(traces, gathered, face_kind, turning):
    rotated = rotate_points(gathered, turning)
    mirror = jnp.concatenate([-traces[0:6], traces[6:9]], axis=0)
    return jnp.where(face_kind == 2, mirror, jnp.where(face_kind == 3, 0.0, rotated))


def face_flux(interior, exterior_trace, interior_material, exterior_material, normals, areas):
    normal = (normals[0], normals[1], normals[2])
    interior_flux = normal_flux(
        interior, interior_material[0], interior_material[1], interior_material[2], normal
    )
    exterior_flux = normal_flux(
        exterior_trace, exterior_material[0], exterior_material[1], exterior_material[2], normal
    )
    interior_speed = jnp.sqrt(
        (interior_material[0] + 2.0 * interior_material[1]) * interior_material[2]
    )
    exterior_speed = jnp.sqrt(
        (exterior_material[0] + 2.0 * exterior_material[1]) * exterior_material[2]
    )
    penalty = 0.5 * jnp.maximum(interior_speed, exterior_speed) * areas
    return 0.5 * (interior_flux + exterior_flux) + penalty * (interior - exterior_trace)


def select_columns(values, picker):
    return jnp.einsum("mqs,st->mqt", values, picker, precision=HIGHEST)


def per_device(
    state,
    geometry,
    material,
    neighbours,
    send_faces,
    vol_eval,
    vol_grad,
    face_eval,
    face_lift,
    normals,
    areas,
):
    elem_count = state.shape[2]
    slot_count = send_faces.shape[2]
    face_total = 4 * elem_count
    traces = jnp.einsum("fbq,mbe->mqfe", face_eval, state, precision=HIGHEST)
    quad_count = traces.shape[1]
    flat_traces = traces.reshape(9, quad_count, face_total)
    listed = send_faces[0].reshape(-1)
    face_ids = jnp.arange(face_total, dtype=jnp.int32)
    send_pick = (face_ids[:, None] == listed[None, :]).astype(jnp.float32)
    outgoing = select_columns(flat_traces, send_pick)
    elem_ids = jnp.arange(elem_count, dtype=jnp.int32)
    elem_pick = (elem_ids[:, None] == (listed % elem_count)[None, :]).astype(jnp.float32)
    sender_material = jnp.dot(material[0:3], elem_pick, precision=HIGHEST)[:, None, :]
    incoming, incoming_material = (
        lax.all_to_all(
            outgoing.astype(jnp.bfloat16), "col", split_axis=2, concat_axis=2, tiled=True
        ).astype(outgoing.dtype),
        lax.all_to_all(
            sender_material.astype(jnp.bfloat16), "col", split_axis=2, concat_axis=2, tiled=True
        ).astype(sender_material.dtype),
    )
    points = jnp.einsum("bq,mbe->mqe", vol_eval, state, precision=HIGHEST).astype(jnp.bfloat16)
    metric = core_and_chips(geometry, (("row_0", "row_1"), "row_2"), (1, 0), 2, 1).astype(
        jnp.float32
    )
    returned = volume_fluxes(points, metric, material)
    volume = jnp.einsum("dbq,dmqe->mbe", vol_grad, returned, preferred_element_type=jnp.float32)
    face_kind = neighbours[0].reshape(-1)
    peer_index = neighbours[1].reshape(-1)
    target = neighbours[2].reshape(-1)
    turning = neighbours[3]
    is_remote = face_kind == 1
    local_source = jnp.where(face_kind == 0, target, face_ids)
    remote_source = peer_index * slot_count + target
    local_pick = (
        (face_ids[:, None] == local_source[None, :]) & jnp.logical_not(is_remote)[None, :]
    ).astype(jnp.float32)
    pool_ids = jnp.arange(incoming.shape[2], dtype=jnp.int32)
    remote_pick = ((pool_ids[:, None] == remote_source[None, :]) & is_remote[None, :]).astype(
        jnp.float32
    )
    gathered = (
        select_columns(flat_traces, local_pick) + select_columns(incoming, remote_pick)
    ).reshape(traces.shape)
    face_material = jnp.broadcast_to(material[0:3][:, None, :], (3, 4, elem_count)).reshape(
        3, face_total
    )
    other_material = jnp.dot(face_material, local_pick, precision=HIGHEST) + jnp.dot(
        incoming_material[:, 0, :], remote_pick, precision=HIGHEST
    )
    other_material = other_material.reshape(3, 1, 4, elem_count)
    exterior_trace = exterior(traces, gathered, neighbours[0], turning)
    numeric_flux = face_flux(
        traces,
        exterior_trace,
        material[0:3][:, None, None, :],
        other_material,
        normals.astype(jnp.float32),
        areas,
    )
    surface = jnp.einsum("fbq,mqfe->mbe", face_lift, numeric_flux, precision=HIGHEST)
    return state + material[3][None, None, :] * (volume - surface)


def solution(mesh):
    finer = Mesh(
        mesh.devices.reshape(4, 4, 2, mesh.shape["col"]), ("row_0", "row_1", "row_2", "col")
    )
    in_specs = (
        P(None, None, COL_ROW),
        P(None, ROW, "col"),
        P(None, COL_ROW),
        P(None, None, COL_ROW),
        P(COL_ROW, None, None),
        P(),
        P(),
        P(),
        P(),
        P(None, None, None, COL_ROW),
        P(None, None, COL_ROW),
    )
    out_specs = P(None, None, COL_ROW)
    return jax.shard_map(
        per_device, mesh=finer, in_specs=in_specs, out_specs=out_specs, check_vma=False
    )
```

profile of v0, /device:TPU:1, one launch (start us, length us, event | category | flops | bytes accessed | tf_op | source)
XLA Modules:
  0.0 91.3 jit_solution(11675323592154055291)
XLA Ops:
  0.0 1.3 %copy.283 = bf16[9,1,32,4,256]{4,3,1,0,2:T(4,128)(2,1)S(1)} copy(bf16[9,1,32,4,256]{4,3,2,1,0:T(4,128)(2,1)} %bitcast.127) | data formatting | bytes 1179648 | tf_op jit(solution)/shard_map/reshape | solution.py:16
  1.3 1.0 %copy.173 = bf16[16,2,9,4,256]{4,0,3,2,1:T(8,128)(2,1)} copy(bf16[16,2,9,4,256]{4,3,2,1,0:T(4,128)(2,1)S(1)} %bitcast.126) | data formatting | bytes 1179648 | tf_op jit(solution)/shard_map/reshape | solution.py:28
  2.3 6.7 %all-to-all-start = ((bf16[16,2,9,4,256]{4,0,3,2,1:T(8,128)(2,1)}), bf16[16,2,9,4,256]{4,0,3,2,1:T(8,128)(2,1)S(1)}, u32[]{:S(2)}, u32[]{:S(2)}) async-start(bf16[16,2,9,4,256]{4,0,3,2,1:T(8,128)(2,1)} %copy.173), calls=%async_computation | async-start | bytes 1179648 | tf_op jit(solution)/shard_map/all_to_all | solution.py:30
  9.0 1.1 %convolution_bitcast_fusion = f32[9,27,4,256]{3,1,2,0:T(8,128)S(1)} fusion(f32[9,35,256]{2,1,0:T(8,128)S(1)} %copy-done.6, f32[4,35,27]{1,0,2:T(4,128)S(1)} %copy-done.12), kind=kOutput, calls=%fused_computation.25 | convolution fusion | flops 104509440 | bytes 1333008 | tf_op jit(solution)/shard_map/fbq,mbe->mqfe/dot_general | solution.py:120
  10.0 1.1 %slice_negate_fusion = f32[6,27,4,256]{3,1,2,0:T(8,128)} fusion(f32[9,27,4,256]{3,1,2,0:T(8,128)S(1)} %convolution_bitcast_fusion), kind=kLoop, calls=%fused_computation.57 | loop fusion | flops 165888 | bytes 1327104 | tf_op jit(solution)/shard_map/neg | solution.py:78
  11.1 0.6 copy.244
  11.8 0.6 compare_bitcast_fusion.3
  12.4 1.5 %reshape.447 = f32[9,27,1024]{2,1,0:T(8,128)} reshape(f32[9,27,4,256]{3,2,1,0:T(4,128)S(1)} %copy.244) | data formatting | bytes 1990656 | tf_op jit(solution)/shard_map/reshape | solution.py:122
  14.1 3.3 %fusion.30 = bf16[9,27,512]{2,1,0:T(8,128)(2,1)} fusion(f32[9,27,1024]{2,1,0:T(8,128)} %reshape.447, s32[512]{0:T(512)S(1)} %reshape_squeeze.9), kind=kOutput, calls=%fused_computation.29 | convolution fusion | flops 1529472512 | bytes 1246208 | tf_op jit(solution)/shard_map/mqs,st->mqt/dot_general | solution.py:101
  17.4 0.6 fusion.107
  18.0 0.3 fusion.61
  18.3 0.9 %copy.242 = bf16[3,1,512]{0,1,2:T(2,128)(2,1)} copy(bf16[3,1,512]{2,0,1:T(4,128)(2,1)S(1)} %fusion.61) | data formatting | bytes 6144 | tf_op jit(solution)/shard_map/convert_element_type | solution.py:135
  19.2 3.0 %fusion.29 = f32[9,128,256]{1,2,0:T(8,128)S(1)} fusion(f32[9,35,256]{2,1,0:T(8,128)} %param.11, f32[35,128]{1,0:T(8,128)S(1)} %copy-done.13), kind=kOutput, calls=%fused_computation.28 | convolution fusion | flops 124452864 | bytes 1520128 | tf_op jit(solution)/shard_map/bq,mbe->mqe/dot_general | solution.py:138
  22.2 4.8 %fusion.4 = f32[9,27,1024]{2,1,0:T(8,128)} fusion(f32[9,27,1024]{2,1,0:T(8,128)} %reshape.447, s32[1024]{0:T(1024)S(1)} %get-tuple-element.76, pred[1024]{0:T(1024)(128)(4,1)S(1)} %not.7), kind=kOutput, calls=%fused_computation.4 | convolution fusion | flops 3059744768 | bytes 1995776 | tf_op jit(solution)/shard_map/mqs,st->mqt/dot_general | solution.py:101
  27.0 6.5 %all-to-all-start.2 = ((bf16[3,1,512]{0,1,2:T(2,128)(2,1)}), bf16[3,1,512]{0,1,2:T(2,128)(2,1)}, u32[]{:S(2)}, u32[]{:S(2)}) async-start(bf16[3,1,512]{0,1,2:T(2,128)(2,1)} %copy.242), calls=%async_computation.2 | async-start | bytes 524288 | tf_op jit(solution)/shard_map/all_to_all | solution.py:134
  33.5 3.8 %copy.245 = bf16[9,27,512]{1,0,2:T(8,128)(2,1)} copy(bf16[9,27,512]{2,1,0:T(8,128)(2,1)} %fusion.30) | data formatting | bytes 497664 | tf_op jit(solution)/shard_map/convert_element_type | solution.py:132
  37.3 3.6 %reshape.484 = bf16[8,2,7776]{2,1,0:T(2,128)(2,1)} reshape(bf16[512,9,27]{2,1,0:T(8,128)(2,1)} %bitcast.121) | data formatting | bytes 497664
  40.9 1.1 %copy.174 = bf16[16,2,9,4,256]{4,3,2,1,0:T(4,128)(2,1)} copy(bf16[16,2,9,4,256]{4,0,3,2,1:T(8,128)(2,1)S(1)} %all-to-all-done) | data formatting | bytes 1179648 | tf_op jit(solution)/shard_map/all_to_all | solution.py:30
  42.0 4.0 %all-to-all-done.2 = bf16[3,1,512]{0,1,2:T(2,128)(2,1)} async-done(((bf16[3,1,512]{0,1,2:T(2,128)(2,1)}), bf16[3,1,512]{0,1,2:T(2,128)(2,1)}, u32[]{:S(2)}, u32[]{:S(2)}) %all-to-all-start.2) | async-done | bytes 3104 | tf_op jit(solution)/shard_map/all_to_all | solution.py:134
  46.0 3.6 %all-to-all-start.3 = ((bf16[8,2,7776]{2,1,0:T(2,128)(2,1)}), bf16[8,2,7776]{2,1,0:T(2,128)(2,1)S(1)}, u32[]{:S(2)}, u32[]{:S(2)}) async-start(bf16[8,2,7776]{2,1,0:T(2,128)(2,1)} %reshape.484), calls=%async_computation.3 | async-start | bytes 499712 | tf_op jit(solution)/shard_map/all_to_all | solution.py:131
  49.6 1.1 %copy.243 = bf16[3,1,512]{2,0,1:T(4,128)(2,1)S(1)} copy(bf16[3,1,512]{0,1,2:T(2,128)(2,1)} %all-to-all-done.2) | data formatting | bytes 6144 | tf_op jit(solution)/shard_map/all_to_all | solution.py:134
  50.7 0.5 fusion.10
  51.2 1.5 %fusion.58 = f32[3,1024]{1,0:T(4,128)S(1)} fusion(f32[3,1024]{1,0:T(4,128)S(1)} %fusion.10, f32[3,1024]{1,0:T(4,128)S(1)} %bitcast.164, s32[1024]{0:T(1024)S(1)} %get-tuple-element.76, pred[1024]{0:T(1024)(128)(4,1)S(1)} %not.7), kind=kOutput, calls=%fused_computation.47 | convolution fusion | flops 39848960 | bytes 41984 | tf_op jit(solution)/shard_map/dot_general | solution.py:164
  52.9 8.0 %all-to-all-done.3 = bf16[8,2,7776]{2,1,0:T(2,128)(2,1)S(1)} async-done(((bf16[8,2,7776]{2,1,0:T(2,128)(2,1)}), bf16[8,2,7776]{2,1,0:T(2,128)(2,1)S(1)}, u32[]{:S(2)}, u32[]{:S(2)}) %all-to-all-start.3) | async-done | bytes 248864 | tf_op jit(solution)/shard_map/all_to_all | solution.py:131
  60.9 6.8 %all-to-all-start.1 = ((bf16[16,2,9,4,256]{4,3,2,1,0:T(4,128)(2,1)}), bf16[16,2,9,4,256]{4,3,2,1,0:T(4,128)(2,1)S(1)}, u32[]{:S(2)}, u32[]{:S(2)}) async-start(bf16[16,2,9,4,256]{4,3,2,1,0:T(4,128)(2,1)} %copy.174), calls=%async_computation.1 | async-start | bytes 1179648 | tf_op jit(solution)/shard_map/all_to_all | solution.py:30
  67.7 2.8 %reshape.485 = bf16[512,9,27]{2,1,0:T(8,128)(2,1)} reshape(bf16[8,2,7776]{2,1,0:T(2,128)(2,1)S(1)} %all-to-all-done.3) | data formatting | bytes 497664
  70.5 2.8 %fusion.25 = f32[9,27,1024]{2,1,0:T(8,128)S(1)} fusion(f32[9,27,1024]{2,1,0:T(8,128)} %fusion.4, bf16[9,27,512]{1,0,2:T(8,128)(2,1)} %bitcast.122, s32[1024]{0:T(1024)S(1)} %get-tuple-element.75, pred[1024]{0:T(1024)(128)(4,1)S(1)} %eq.123), kind=kOutput, calls=%fused_computation.24 | convolution fusion | flops 256101376 | bytes 2244608 | tf_op jit(solution)/shard_map/mqs,st->mqt/dot_general | solution.py:101
  73.3 1.4 %reshape.448 = f32[9,27,4,256]{3,2,1,0:T(4,128)} reshape(f32[9,27,1024]{2,1,0:T(8,128)S(1)} %fusion.25) | data formatting | bytes 1990656 | tf_op jit(solution)/shard_map/reshape | solution.py:160
  74.8 1.4 %reshape_reshape.3 = f32[9,9,3,4,256]{4,3,2,1,0:T(4,128)} reshape(f32[9,27,1024]{2,1,0:T(8,128)S(1)} %fusion.25) | data formatting | bytes 1990656 | tf_op jit(solution)/shard_map/reshape;reshape | solution.py:70
  76.2 1.3 %fusion.106 = (f32[9,9,1,4,256]{4,3,2,1,0:T(4,128)S(1)}, f32[9,9,1,4,256]{4,3,2,1,0:T(4,128)S(1)}) fusion(f32[9,9,3,4,256]{4,3,2,1,0:T(4,128)} %reshape_reshape.3), kind=kLoop, calls=%fused_computation.201 | loop fusion | bytes 1327104 | tf_op jit(solution)/shard_map/jit(_roll_static)/slice | solution.py:71
  77.5 0.1 copy-done.3
  77.6 0.2 fusion.105
  77.8 0.5 pad_maximum_fusion
  78.3 1.0 %slice-done = f32[3,27,4,256]{3,1,2,0:T(8,128)S(1)} async-done(((f32[9,27,4,256]{3,1,2,0:T(8,128)}), f32[3,27,4,256]{3,1,2,0:T(8,128)S(1)}, s32[]{:S(2)}) %slice-start) | async-done | bytes 331800 | tf_op jit(solution)/shard_map/slice | solution.py:41
  79.4 0.8 maximum_select_fusion
  80.4 1.1 %copy-done.2 = f32[9,27,4,256]{3,1,2,0:T(8,128)S(1)} copy-done((f32[9,27,4,256]{3,1,2,0:T(8,128)S(1)}, f32[9,27,4,256]{3,1,2,0:T(8,128)}, u32[]{:S(2)}) %copy-start.2) | copy-done | bytes 995352
  82.1 0.6 copy-done.11
  82.7 1.8 %convolution_bitcast_fusion.1 = f32[9,256,35]{1,2,0:T(8,128)} fusion(f32[9,27,4,256]{3,1,2,0:T(8,128)S(1)} %copy-done.2, f32[9,27,4,256]{3,1,2,0:T(8,128)S(1)} %maximum_select_fusion, f32[9,27,4,256]{3,1,2,0:T(8,128)S(1)} %fusion.84, f32[9,27,4,256]{3,1,2,0:T(8,128)S(1)} %get-tuple-element.54, f32[27,4,256]{2,0,1:T(8,128)S(1)} %copy.250, ...), kind=kOutput, calls=%fused_computation.30 | convolution fusion | flops 105753600 | bytes 4429584 | tf_op jit(solution)/shard_map/fbq,mqfe->mbe/dot_general | solution.py:177
  84.6 0.2 bitcast_convert_fusion
  84.8 0.3 copy.282
  85.1 0.8 fusion.104
  86.8 0.1 constant_dynamic-update-slice_fusion.8
  87.1 0.2 constant_dynamic-update-slice_fusion.6
  87.4 0.2 constant_dynamic-update-slice_fusion.15
  87.7 0.1 constant_dynamic-update-slice_fusion.3
  88.4 0.1 constant_dynamic-update-slice_fusion.10
  89.0 0.7 copy-done.7
  89.8 1.6 %fusion.45 = f32[9,35,256]{2,1,0:T(8,128)} fusion(f32[9,35,256]{2,1,0:T(8,128)S(1)} %copy-done.7, f32[9,256,35]{1,2,0:T(8,128)S(1)} %copy-done.8, bf16[1,9,128,256]{2,3,1,0:T(8,128)(2,1)S(1)} %bitcast.168, bf16[1,9,128,256]{2,3,1,0:T(8,128)(2,1)S(1)} %bitcast.169, bf16[1,9,128,256]{2,3,1,0:T(8,128)(2,1)S(1)} %bitcast.170, f32[256]{0:T(256)S(1)} %bitcast.172, ...), kind=kOutput, calls=%fused_computation.35 | convolution fusion | flops 63942912 | bytes 2765056 | tf_op jit(solution)/shard_map/dbq,dmqe->mbe/dot_general | solution.py:143
  (96 shorter events, 3.5 us)
Async XLA Ops:
  0.0 89.0 %copy-start = (bf16[3,35,128]{2,1,0:T(8,128)(2,1)S(1)}, bf16[3,35,128]{2,1,0:T(8,128)(2,1)}, u32[]{:S(2)}) copy-start(bf16[3,35,128]{2,1,0:T(8,128)(2,1)} %param.17) | copy-start | bytes 80644
  1.3 7.7 %copy-start.6 = (f32[9,35,256]{2,1,0:T(8,128)S(1)}, f32[9,35,256]{2,1,0:T(8,128)}, u32[]{:S(2)}) copy-start(f32[9,35,256]{2,1,0:T(8,128)} %param.11) | copy-start | bytes 967684
  1.3 7.7 %copy-start.12 = (f32[4,35,27]{1,0,2:T(4,128)S(1)}, f32[4,35,27]{1,0,2:T(4,128)}, u32[]{:S(2)}) copy-start(f32[4,35,27]{1,0,2:T(4,128)} %param.18) | copy-start | bytes 45364
  2.3 24.8 %all-to-all-start = ((bf16[16,2,9,4,256]{4,0,3,2,1:T(8,128)(2,1)}), bf16[16,2,9,4,256]{4,0,3,2,1:T(8,128)(2,1)S(1)}, u32[]{:S(2)}, u32[]{:S(2)}) async-start(bf16[16,2,9,4,256]{4,0,3,2,1:T(8,128)(2,1)} %copy.173), calls=%async_computation | async-start | bytes 1179648 | tf_op jit(solution)/shard_map/all_to_all | solution.py:30
  10.0 23.5 %copy-start.1 = (f32[9,27,4,256]{3,1,2,0:T(8,128)}, f32[9,27,4,256]{3,1,2,0:T(8,128)S(1)}, u32[]{:S(2)}) copy-start(f32[9,27,4,256]{3,1,2,0:T(8,128)S(1)} %convolution_bitcast_fusion) | copy-start | bytes 2985988
  11.1 0.7 copy-start.14
  11.8 2.2 %copy-start.16 = (s32[1,8,64]{2,1,0:T(8,128)S(1)}, s32[1,8,64]{2,1,0:T(8,128)}, u32[]{:S(2)}) copy-start(s32[1,8,64]{2,1,0:T(8,128)} %param.15) | copy-start | bytes 6148
  14.0 3.4 %copy-start.15 = (f32[4,256]{1,0:T(4,128)S(1)}, f32[4,256]{1,0:T(4,128)}, u32[]{:S(2)}) copy-start(f32[4,256]{1,0:T(4,128)} %param.13) | copy-start | bytes 12292
  14.0 4.0 %copy-start.9 = (bf16[3,27,4,256]{3,2,1,0:T(4,128)(2,1)S(1)}, bf16[3,27,4,256]{3,2,1,0:T(4,128)(2,1)}, u32[]{:S(2)}) copy-start(bf16[3,27,4,256]{3,2,1,0:T(4,128)(2,1)} %param.20) | copy-start | bytes 497668
  14.1 5.1 %copy-start.13 = (f32[35,128]{1,0:T(8,128)S(1)}, f32[35,128]{1,0:T(8,128)}, u32[]{:S(2)}) copy-start(f32[35,128]{1,0:T(8,128)} %param.16) | copy-start | bytes 53764
  27.0 18.9 %all-to-all-start.2 = ((bf16[3,1,512]{0,1,2:T(2,128)(2,1)}), bf16[3,1,512]{0,1,2:T(2,128)(2,1)}, u32[]{:S(2)}, u32[]{:S(2)}) async-start(bf16[3,1,512]{0,1,2:T(2,128)(2,1)} %copy.242), calls=%async_computation.2 | async-start | bytes 524288 | tf_op jit(solution)/shard_map/all_to_all | solution.py:134
  46.0 14.9 %all-to-all-start.3 = ((bf16[8,2,7776]{2,1,0:T(2,128)(2,1)}), bf16[8,2,7776]{2,1,0:T(2,128)(2,1)S(1)}, u32[]{:S(2)}, u32[]{:S(2)}) async-start(bf16[8,2,7776]{2,1,0:T(2,128)(2,1)} %reshape.484), calls=%async_computation.3 | async-start | bytes 499712 | tf_op jit(solution)/shard_map/all_to_all | solution.py:131
  51.2 1.6 %copy-start.10 = (f32[27,4,256]{2,1,0:T(4,128)S(1)}, f32[27,4,256]{2,1,0:T(4,128)}, u32[]{:S(2)}) copy-start(f32[27,4,256]{2,1,0:T(4,128)} %param.21) | copy-start | bytes 331780
  60.9 23.7 %all-to-all-start.1 = ((bf16[16,2,9,4,256]{4,3,2,1,0:T(4,128)(2,1)}), bf16[16,2,9,4,256]{4,3,2,1,0:T(4,128)(2,1)S(1)}, u32[]{:S(2)}, u32[]{:S(2)}) async-start(bf16[16,2,9,4,256]{4,3,2,1,0:T(4,128)(2,1)} %copy.174), calls=%async_computation.1 | async-start | bytes 1179648 | tf_op jit(solution)/shard_map/all_to_all | solution.py:30
  76.2 1.4 %copy-start.3 = (f32[9,9,3,4,256]{4,3,2,1,0:T(4,128)S(1)}, f32[9,9,3,4,256]{4,3,2,1,0:T(4,128)}, u32[]{:S(2)}) copy-start(f32[9,9,3,4,256]{4,3,2,1,0:T(4,128)} %reshape_reshape.3) | copy-start | bytes 2985988
  77.8 1.5 %slice-start = ((f32[9,27,4,256]{3,1,2,0:T(8,128)}), f32[3,27,4,256]{3,1,2,0:T(8,128)S(1)}, s32[]{:S(2)}) async-start(f32[9,27,4,256]{3,1,2,0:T(8,128)} %copy-done.1), calls=%async_computation.4 | async-start | bytes 786432 | tf_op jit(solution)/shard_map/slice | solution.py:41
  77.8 1.5 %copy-start.4 = (f32[9,27,4,256]{3,2,1,0:T(4,128)S(1)}, f32[9,27,4,256]{3,2,1,0:T(4,128)}, u32[]{:S(2)}) copy-start(f32[9,27,4,256]{3,2,1,0:T(4,128)} %reshape.448) | copy-start | bytes 2985988
  77.8 1.5 %copy-start.5 = (f32[6,27,4,256]{3,1,2,0:T(8,128)S(1)}, f32[6,27,4,256]{3,1,2,0:T(8,128)}, u32[]{:S(2)}) copy-start(f32[6,27,4,256]{3,1,2,0:T(8,128)} %slice_negate_fusion) | copy-start | bytes 1990660
  77.8 1.5 %copy-start.17 = (pred[4,256]{1,0:T(4,128)(4,1)S(1)}, pred[4,256]{1,0:T(4,128)(4,1)}, u32[]{:S(2)}) copy-start(pred[4,256]{1,0:T(4,128)(4,1)} %get-tuple-element.61) | copy-start | bytes 3076
  77.8 1.5 %copy-start.18 = (pred[4,256]{1,0:T(4,128)(4,1)S(1)}, pred[4,256]{1,0:T(4,128)(4,1)}, u32[]{:S(2)}) copy-start(pred[4,256]{1,0:T(4,128)(4,1)} %get-tuple-element.62) | copy-start | bytes 3076
  77.8 1.5 %copy-start.19 = (pred[4,256]{1,0:T(4,128)(4,1)S(1)}, pred[4,256]{1,0:T(4,128)(4,1)}, u32[]{:S(2)}) copy-start(pred[4,256]{1,0:T(4,128)(4,1)} %get-tuple-element.64) | copy-start | bytes 3076
  80.2 1.3 %copy-start.2 = (f32[9,27,4,256]{3,1,2,0:T(8,128)S(1)}, f32[9,27,4,256]{3,1,2,0:T(8,128)}, u32[]{:S(2)}) copy-start(f32[9,27,4,256]{3,1,2,0:T(8,128)} %copy-done.1) | copy-start | bytes 2985988
  81.9 0.8 copy-start.11
  88.7 1.0 %copy-start.7 = (f32[9,35,256]{2,1,0:T(8,128)S(1)}, f32[9,35,256]{2,1,0:T(8,128)}, u32[]{:S(2)}) copy-start(f32[9,35,256]{2,1,0:T(8,128)} %param.11) | copy-start | bytes 967684
  88.7 1.1 %copy-start.8 = (f32[9,256,35]{1,2,0:T(8,128)S(1)}, f32[9,256,35]{1,2,0:T(8,128)}, u32[]{:S(2)}) copy-start(f32[9,256,35]{1,2,0:T(8,128)} %convolution_bitcast_fusion.1) | copy-start | bytes 967684
  88.7 1.1 %copy-start.20 = (f32[1,256]{1,0:T(1,128)S(1)}, f32[1,256]{1,0:T(1,128)}, u32[]{:S(2)}) copy-start(f32[1,256]{1,0:T(1,128)} %get-tuple-element.67) | copy-start | bytes 3076
where the time goes:
time: 92.4 us; the launch traced here: 91.3 us
  local copies, waits for them, and re-layouts  28 us (30%)
  starting transfers between devices  23.5 us (25%)
  matrix products  20.7 us (22%)
  waiting for transfers between devices  12 us (13%)
  other arithmetic  6.65 us (7%)
    all_to_all x2, starting transfers between devices, turned_blocks(): result = lax.all_to_all(result, axes[k], k, k, tiled=True)  13.4 us
    dot_general x3, matrix products, select_columns(): return jnp.einsum('mqs,st->mqt', values, picker, precision=HIGHEST)  10.9 us
    unnamed x48, local copies, waits for them, and re-layouts  9.2 us
    all_to_all x1, waiting for transfers between devices, per_device(): lax.all_to_all(outgoing.astype(jnp.bfloat16), 'col', split_axis=2, concat...  8 us
    all_to_all x1, starting transfers between devices, per_device(): lax.all_to_all(sender_material.astype(jnp.bfloat16), 'col', split_axis=2,...  6.47 us
    all_to_all x1, waiting for transfers between devices, per_device(): lax.all_to_all(sender_material.astype(jnp.bfloat16), 'col', split_axis=2,...  4 us
    convert_element_type x1, local copies, waits for them, and re-layouts, per_device(): outgoing.astype(jnp.bfloat16)  3.75 us
    all_to_all x1, starting transfers between devices, per_device(): lax.all_to_all(outgoing.astype(jnp.bfloat16), 'col', split_axis=2, concat...  3.59 us
  transfers between devices with their start and end apart: 4, of which 2 were waited for; matrix products, arithmetic and copies ran while one was open for 48% of the time, Pallas kernels for 0%

commit v1 on v0

v1 whole, which is shorter than its diff:
```python
import jax
import jax.numpy as jnp
from jax import lax
from jax.experimental import pallas as pl
from jax.experimental.pallas import tpu as pltpu
from jax.sharding import PartitionSpec as P

MESH = pl.DeviceIdType.MESH
F32, BF16, I32 = jnp.float32, jnp.bfloat16, jnp.int32

NQ, NB, BP = 9, 35, 40
FQ, FACES, E = 27, 4, 256
ROWS, COLS, SLOTS = 32, 8, 64
LANES = 128
WIDE = NQ * LANES
KP = NQ * BP + 8
PITCH = 264


def iota(shape, dim):
    return lax.broadcasted_iota(I32, shape, dim)


def ones_where(mask):
    return jnp.where(mask, 1.0, 0.0).astype(BF16)


def mm(a, b):
    return jnp.dot(a, b, preferred_element_type=F32)


def mm_t(a, b):
    return lax.dot_general(a, b, (((1,), (1,)), ((), ())), preferred_element_type=F32)


def halves(x):
    return jnp.concatenate([x[:, :LANES], x[:, LANES:]], axis=0)


def steps(x, size, count):
    result = jnp.zeros_like(x)
    for k in range(1, count):
        result = result + jnp.where(x >= size * k, 1, 0)
    return result


def kernel(
    state, geometry, material, neighbours, send_faces, vol_eval, vol_grad, face_eval, face_lift,
    normals, areas, out,
    st_v, mat_v, nb_v, sf_v, ve_v, vg_v, fe_v, fl_v, nrm_v, ar_v,
    recv, sendb, xr, sp, sb, raw, ohs, tr, pts, own, gath, flx, fx, vgm,
    load_sem, gsend_sem, grecv_sem, tsend_sem, trecv_sem,
):
    row, col = lax.axis_index("row"), lax.axis_index("col")
    chip, core = row // 2, row % 2
    cx, cy = chip // 4, chip % 4

    pairs = [
        (state, st_v), (material, mat_v), (neighbours, nb_v), (send_faces, sf_v), (vol_eval, ve_v),
        (vol_grad, vg_v), (face_eval, fe_v), (face_lift, fl_v), (normals, nrm_v), (areas, ar_v),
    ]
    loads = [pltpu.make_async_copy(a, b, load_sem.at[i]) for i, (a, b) in enumerate(pairs)]
    for copy in loads:
        copy.start()

    def block(p):
        return geometry.at[:, pl.ds(2 * p, 2)]

    local = pltpu.make_async_copy(block(row), recv.at[row], grecv_sem.at[row])
    local.start()

    barrier = pltpu.get_barrier_semaphore()

    @pl.loop(1, ROWS)
    def _(d):
        pl.semaphore_signal(
            barrier, inc=1, device_id={"row": lax.rem(row + d, ROWS), "col": col}, device_id_type=MESH
        )

    @pl.loop(1, COLS)
    def _(d):
        pl.semaphore_signal(
            barrier, inc=1, device_id={"row": row, "col": lax.rem(col + d, COLS)}, device_id_type=MESH
        )

    def metric_copy(to, source):
        return pltpu.make_async_remote_copy(
            src_ref=block(to), dst_ref=recv.at[source], send_sem=gsend_sem.at[to],
            recv_sem=grecv_sem.at[source], device_id={"row": to, "col": col}, device_id_type=MESH,
        )

    def trace_copy(to, source):
        return pltpu.make_async_remote_copy(
            src_ref=sendb.at[to], dst_ref=xr.at[source], send_sem=tsend_sem.at[to],
            recv_sem=trecv_sem.at[source], device_id={"row": row, "col": to}, device_id_type=MESH,
        )

    def chip_at(o, sign):
        dx, dy = o // 4, o % 4
        return lax.rem(cx + sign * dx + 4, 4) * 4 + lax.rem(cy + sign * dy + 4, 4)

    for copy in loads:
        copy.wait()
    for m in range(NQ):
        sp[m * BP : m * BP + NB, :] = st_v[m]
        sp[m * BP + NB : (m + 1) * BP, :] = jnp.zeros((BP - NB, E), F32)
    high = mat_v[0:3, :].astype(BF16).astype(F32)
    sp[NQ * BP : NQ * BP + 3, :] = high
    sp[NQ * BP + 3 : NQ * BP + 6, :] = mat_v[0:3, :] - high
    sp[NQ * BP + 6 : KP, :] = jnp.zeros((2, E), F32)
    dof = sp[...].astype(BF16)

    raw[...] = jnp.zeros(raw.shape, F32)
    for q in range(FQ):
        for t in range(2):
            raw[0, 8 * q + 4 * t : 8 * q + 4 * t + 4, 0:NB] = fe_v[q]
            raw[1, 8 * q + 4 * t : 8 * q + 4 * t + 4, 0:NB] = fl_v[q]
    eval_rows = raw[0].astype(BF16)
    lift_rows = raw[1].astype(BF16)

    col_kp = iota((1, KP), 1)
    m_col = steps(col_kp, BP, NQ)
    spread9 = ones_where((iota((BP, 1), 0) == col_kp - BP * m_col) & (col_kp < NQ * BP))
    wide_eval = mm(eval_rows, spread9).astype(BF16)
    row_t = iota((256, 1), 0)
    m_row = steps(row_t, FQ, NQ)
    q_row = row_t - FQ * m_row
    same = (m_row == m_col) & (row_t < NQ * FQ) & (col_kp < NQ * BP)
    carry = (row_t - NQ * FQ == col_kp - NQ * BP) & (col_kp >= NQ * BP)
    for f in range(FACES):
        pick = ones_where(iota((1, 8 * FQ), 1) == 8 * q_row + f)
        weights = jnp.where(same, mm(pick, wide_eval), jnp.where(carry, 1.0, 0.0)).astype(BF16)
        tr[:, f * E : (f + 1) * E] = mm(weights, dof).astype(BF16)

    listed = jnp.transpose(jnp.concatenate([sf_v[0], sf_v[0]], axis=1))
    for p in range(COLS):
        ohs[p * SLOTS : (p + 1) * SLOTS, :] = ones_where(
            listed[0:SLOTS, p : p + 1] == iota((1, FACES * E), 1)
        )
    outgoing = mm_t(ohs[...], tr[...]).astype(BF16)
    for p in range(COLS):
        sendb[p] = outgoing[p * SLOTS : (p + 1) * SLOTS, :]
    xr[col] = jnp.zeros((SLOTS, 256), BF16)

    pl.semaphore_wait(barrier, ROWS + COLS - 2)

    metric_copy(2 * chip + (1 - core), row).start()

    @pl.loop(1, 16)
    def _(o):
        peer = chip_at(o, 1)
        metric_copy(2 * peer + core, row).start()
        metric_copy(2 * peer + (1 - core), row).start()

    @pl.loop(1, COLS)
    def _(d):
        trace_copy(lax.rem(col + d, COLS), col).start()

    for m in range(NQ):
        both = jnp.concatenate(
            [sp[m * BP : (m + 1) * BP, :LANES], sp[m * BP : (m + 1) * BP, LANES:]], axis=0
        )
        sb[:, m * LANES : (m + 1) * LANES] = both.astype(BF16)
    tile_col = jnp.where(iota((1, 2 * BP), 1) >= BP, 1, 0)
    twice = ones_where(iota((BP, 1), 0) == iota((1, 2 * BP), 1) - BP * tile_col)
    face_row = iota((8 * FQ, 1), 0)
    eval_mask = ((face_row >> 2) & 1) == tile_col
    face_weights = jnp.where(eval_mask, mm(eval_rows, twice), 0.0).astype(BF16)
    own[...] = mm(face_weights, sb[...]).reshape(FQ, 8, WIDE)
    point_row = iota((256, 1), 0)
    spread_v = ones_where(iota((1, 128), 1) == 4 * (point_row >> 3) + (point_row & 3))
    pad = jnp.zeros((BP - NB, 128), F32)
    eval2 = jnp.concatenate([ve_v[...], pad, ve_v[...], pad], axis=0).astype(BF16)
    vol_mask = ((point_row >> 2) & 1) == tile_col
    vol_weights = jnp.where(vol_mask, mm_t(spread_v, eval2), 0.0).astype(BF16)
    pts[...] = mm(vol_weights, sb[...])
    tile_row = jnp.where(iota((2 * BP, 1), 0) >= BP, 1, 0)
    grad_mask = tile_row == ((iota((1, 256), 1) >> 2) & 1)
    for d in range(3):
        grad = vg_v[d].astype(F32)
        grad2 = jnp.concatenate([grad, pad, grad, pad], axis=0).astype(BF16)
        vgm[:, d * 256 : (d + 1) * 256] = jnp.where(grad_mask, mm_t(grad2, spread_v), 0.0).astype(BF16)
    twice_t = ones_where(iota((2 * BP, 1), 0) - BP * tile_row == iota((1, BP), 1))
    lift_mask = tile_row == ((iota((1, 8 * FQ), 1) >> 2) & 1)
    lift = jnp.where(lift_mask, mm_t(twice_t, lift_rows), 0.0).astype(BF16)

    kind, peer, target, turn = nb_v[0], nb_v[1], nb_v[2], nb_v[3]
    face_id = iota((FACES, E), 0) * E + iota((FACES, E), 1)
    code = jnp.where(
        kind == 0, target, jnp.where(kind == 1, FACES * E + peer * SLOTS + target, face_id)
    )
    for f in range(FACES):
        got = mm(tr[...], ones_where(iota((FACES * E, 1), 0) == code[f : f + 1, :]))
        for t in range(2):
            gath[(4 * t + f) * PITCH : (4 * t + f) * PITCH + 256, :] = got[:, t * LANES : (t + 1) * LANES]

    @pl.loop(1, COLS)
    def _(d):
        source = lax.rem(col + COLS - d, COLS)
        trace_copy(source, source).wait_recv()

    ident = ones_where(iota((256, 1), 0) == iota((1, 256), 1))
    xt = mm_t(ident, xr[...].reshape(COLS * SLOTS, 256)).astype(BF16)
    for f in range(FACES):
        got = mm(xt, ones_where(iota((COLS * SLOTS, 1), 0) + FACES * E == code[f : f + 1, :]))
        for t in range(2):
            at = (4 * t + f) * PITCH
            gath[at : at + 256, :] = gath[at : at + 256, :] + got[:, t * LANES : (t + 1) * LANES]

    def gathered(r):
        return gath[pl.ds(r, 8, stride=PITCH), :]

    def per_face(i):
        return jnp.concatenate(
            [jnp.broadcast_to(mat_v[i : i + 1, t * LANES : (t + 1) * LANES], (4, LANES)) for t in range(2)],
            axis=0,
        )

    kind8, turn8 = halves(kind), halves(turn)
    l1, g1, w1 = per_face(0), per_face(1), per_face(2)
    l2, g2, w2 = [gathered(NQ * FQ + i) + gathered(NQ * FQ + 3 + i) for i in range(3)]
    fastest = 0.5 * jnp.maximum(jnp.sqrt((l1 + 2.0 * g1) * w1), jnp.sqrt((l2 + 2.0 * g2) * w2))
    sign_v = jnp.where(kind8 == 3, 0.0, 1.0)
    sign_s = jnp.where(kind8 == 2, -1.0, sign_v)
    l1, g1, w1 = 0.5 * l1, 0.5 * g1, 0.5 * w1
    l2, g2, w2 = 0.5 * l2 * sign_v, 0.5 * g2 * sign_v, 0.5 * w2 * sign_s
    turn_one, turn_two = turn8 == 1, turn8 == 2

    @pl.loop(0, FQ // 3)
    def _(i):
        q0 = 3 * i
        outer = [[], [], []]
        for m in range(NQ):
            g = [gathered(m * FQ + q0 + k) for k in range(3)]
            for k in range(3):
                outer[k].append(
                    jnp.where(turn_one, g[(k + 1) % 3], jnp.where(turn_two, g[(k + 2) % 3], g[k]))
                )
        for k in range(3):
            q = q0 + k
            o = outer[k]
            u = [own[q, :, m * LANES : (m + 1) * LANES] for m in range(NQ)]
            n = [halves(nrm_v[j, q].astype(F32)) for j in range(3)]
            penalty = fastest * halves(ar_v[q])
            rigid = [g1 * u[6 + j] + g2 * o[6 + j] for j in range(3)]
            lame = [l1 * u[6 + j] + l2 * o[6 + j] for j in range(3)]
            stress = [w1 * u[s] + w2 * o[s] for s in range(6)]
            pressure = n[0] * lame[0] + n[1] * lame[1] + n[2] * lame[2]
            flux = [
                pressure + 2.0 * (n[0] * rigid[0]),
                pressure + 2.0 * (n[1] * rigid[1]),
                pressure + 2.0 * (n[2] * rigid[2]),
                n[0] * rigid[1] + n[1] * rigid[0],
                n[1] * rigid[2] + n[2] * rigid[1],
                n[0] * rigid[2] + n[2] * rigid[0],
                stress[0] * n[0] + stress[3] * n[1] + stress[5] * n[2],
                stress[3] * n[0] + stress[1] * n[1] + stress[4] * n[2],
                stress[5] * n[0] + stress[4] * n[1] + stress[2] * n[2],
            ]
            for m in range(NQ):
                sign = sign_s if m < 6 else sign_v
                flx[q, :, m * LANES : (m + 1) * LANES] = penalty * (u[m] - sign * o[m]) - flux[m]

    surface = mm(lift, flx[...].reshape(8 * FQ, WIDE).astype(BF16))

    @pl.loop(0, 16)
    def _(o):
        src = chip_at(o, -1)
        for a in range(2):
            metric_copy(2 * src + a, 2 * src + a).wait_recv()
        at = pl.multiple_of(16 * src, 16)
        u = [pts[pl.ds(at, 16), m * LANES : (m + 1) * LANES] for m in range(NQ)]
        for d in range(3):
            n = [
                jnp.concatenate(
                    [got8(recv, 2 * src, 3 * d + j), got8(recv, 2 * src + 1, 3 * d + j)], axis=0
                )
                for j in range(3)
            ]
            product = [
                n[0] * u[6],
                n[1] * u[7],
                n[2] * u[8],
                n[0] * u[7] + n[1] * u[6],
                n[1] * u[8] + n[2] * u[7],
                n[0] * u[8] + n[2] * u[6],
                u[0] * n[0] + u[3] * n[1] + u[5] * n[2],
                u[3] * n[0] + u[1] * n[1] + u[4] * n[2],
                u[5] * n[0] + u[4] * n[1] + u[2] * n[2],
            ]
            for m in range(NQ):
                fx[pl.ds(pl.multiple_of(d * 256 + at, 16), 16), m * LANES : (m + 1) * LANES] = product[
                    m
                ].astype(BF16)

    volume = mm(vgm[...], fx[...])
    for t in range(2):
        rows = slice(t * BP, (t + 1) * BP)
        lanes = slice(t * LANES, (t + 1) * LANES)
        v = [volume[rows, m * LANES : (m + 1) * LANES] for m in range(NQ)]
        l, g, w, step = [mat_v[i : i + 1, lanes] for i in range(4)]
        pressure = l * (v[0] + v[1] + v[2])
        for m in range(NQ):
            if m < 3:
                total = -(pressure + 2.0 * g * v[m])
            elif m < 6:
                total = -g * v[m]
            else:
                total = -w * v[m]
            total = total - surface[rows, m * LANES : (m + 1) * LANES]
            out[m, :, lanes] = st_v[m, :, lanes] + (step * total)[0:NB]

    @pl.loop(1, ROWS)
    def _(d):
        to = lax.rem(row + d, ROWS)
        metric_copy(to, row).wait_send()

    @pl.loop(1, COLS)
    def _(d):
        to = lax.rem(col + d, COLS)
        trace_copy(to, col).wait_send()


def got8(recv, r, k):
    return recv[r, k].astype(F32).reshape(8, LANES)


def per_device(
    state, geometry, material, neighbours, send_faces, vol_eval, vol_grad, face_eval, face_lift,
    normals, areas,
):
    geometry = jnp.transpose(geometry.reshape(9, 4, 2 * ROWS, LANES), (0, 2, 1, 3))
    face_eval = jnp.transpose(face_eval, (2, 0, 1))
    face_lift = jnp.transpose(face_lift, (2, 0, 1))
    args = (
        state, geometry, material, neighbours, send_faces, vol_eval, vol_grad, face_eval, face_lift,
        normals, areas,
    )
    staged = [a for i, a in enumerate(args) if i != 1]
    dma = pltpu.SemaphoreType.DMA
    return pl.pallas_call(
        kernel,
        out_shape=jax.ShapeDtypeStruct((NQ, NB, E), F32),
        in_specs=[pl.BlockSpec(memory_space=pl.ANY)] * len(args),
        out_specs=pl.BlockSpec(memory_space=pltpu.VMEM),
        scratch_shapes=[pltpu.VMEM(a.shape, a.dtype) for a in staged]
        + [
            pltpu.VMEM((ROWS, 9, 2, 4, LANES), BF16),
            pltpu.VMEM((COLS, SLOTS, 256), BF16),
            pltpu.VMEM((COLS, SLOTS, 256), BF16),
            pltpu.VMEM((KP, E), F32),
            pltpu.VMEM((2 * BP, WIDE), BF16),
            pltpu.VMEM((2, 8 * FQ, BP), F32),
            pltpu.VMEM((COLS * SLOTS, FACES * E), BF16),
            pltpu.VMEM((256, FACES * E), BF16),
            pltpu.VMEM((256, WIDE), F32),
            pltpu.VMEM((FQ, 8, WIDE), F32),
            pltpu.VMEM((8 * PITCH, LANES), F32),
            pltpu.VMEM((FQ, 8, WIDE), F32),
            pltpu.VMEM((3 * 256, WIDE), BF16),
            pltpu.VMEM((2 * BP, 3 * 256), BF16),
            dma((len(staged),)), dma((ROWS,)), dma((ROWS,)), dma((COLS,)), dma((COLS,)),
        ],
        compiler_params=pltpu.CompilerParams(
            collective_id=0, has_side_effects=True, vmem_limit_bytes=60 * 1024 * 1024
        ),
        name="section",
    )(*args)


def solution(mesh):
    blocks = P(None, None, ("col", "row"))
    in_specs = (
        blocks, P(None, "row", "col"), P(None, ("col", "row")), blocks, P(("col", "row"), None, None),
        P(), P(), P(), P(), P(None, None, None, ("col", "row")), blocks,
    )
    return jax.shard_map(
        per_device, mesh=mesh, in_specs=in_specs, out_specs=blocks, check_vma=False
    )
```

time: 92.4 us -> 27 us (0.29); the launches traced: 91.3 us -> 26.9 us
  local copies, waits for them, and re-layouts: 28 us -> 1.75 us
  Pallas kernels: 0 us -> 25.1 us
  starting transfers between devices: 23.5 us -> 0 us
  matrix products: 20.7 us -> 0 us
  waiting for transfers between devices: 12 us -> 0 us
  other arithmetic: 6.65 us -> 0 us
    pallas_call x0 -> x1, Pallas kernels: none -> 25.1 us  [per_device(): pl.pallas_call(kernel, out_shape=jax.ShapeDtypeStruct((NQ, NB, E), F32),...]
    all_to_all x4 -> x0, starting transfers between devices: 23.5 us -> none  [the longest x2 13.4 us: turned_blocks(): result = lax.all_to_all(result, axes[k], k, k, tiled=True)]
    dot_general x10 -> x0, matrix products: 20.7 us -> none  [the longest x3 10.9 us: select_columns(): return jnp.einsum('mqs,st->mqt', values, picker, precision=HIGHEST)]
    all_to_all x4 -> x0, waiting for transfers between devices: 12 us -> none  [the longest x1 8 us: per_device(): lax.all_to_all(outgoing.astype(jnp.bfloat16), 'col', split_axis=2, concat...]
    unnamed x48 -> x1, local copies, waits for them, and re-layouts: 9.2 us -> 1.75 us
    reshape x4 -> x0, local copies, waits for them, and re-layouts: 5.19 us -> none  [the longest x1 1.54 us: per_device(): flat_traces = traces.reshape(9, quad_count, face_total)]
    convert_element_type x3 -> x0, local copies, waits for them, and re-layouts: 5 us -> none  [the longest x1 3.75 us: per_device(): outgoing.astype(jnp.bfloat16)]
    slice x14 -> x0, local copies, waits for them, and re-layouts: 4.16 us -> none  [the longest x2 1.48 us: rotate_points(): rotated_one = jnp.roll(grouped, -1, axis=2).reshape(full_shape)]
  transfers between devices with their start and end apart: 4 -> 0, of which waited for: 2 -> 0; matrix products, arithmetic and copies ran while one was open for 48% -> 0% of each run, Pallas kernels for 0% -> 0%
where the time goes in v1:
time: 27 us; the launch traced here: 26.9 us
  Pallas kernels  25.1 us (93%)
  local copies, waits for them, and re-layouts  1.75 us (6%)
    pallas_call x1, Pallas kernels, per_device(): pl.pallas_call(kernel, out_shape=jax.ShapeDtypeStruct((NQ, NB, E), F32),...  25.1 us
    unnamed x1, local copies, waits for them, and re-layouts  1.75 us

profile of v1, /device:TPU:1, one launch (start us, length us, event | category | flops | bytes accessed | tf_op | source)
XLA Modules:
  0.0 26.9 jit_solution(11992761610204817035)
XLA Ops:
  0.0 25.1 %section.1 = f32[9,35,256]{2,1,0:T(8,128)} custom-call(f32[9,35,256]{2,1,0:T(8,128)} %state.1, bf16[9,64,4,128]{3,2,1,0:T(4,128)(2,1)} %bitcast.5, f32[4,256]{1,0:T(4,128)} %material.1, s32[4,4,256]{2,1,0:T(4,128)} %neighbours.1, s32[1,8,64]{2,1,0:T(8,128)} %send_faces.1, f32[35,128]{1,0:T(8,128)} %vol_eval.1, bf16[3,35,128]{2,1,0:T(8,128)(2,1)} %vol_grad.1, ...), custom_call_target="tpu_custom_call" | custom-call | tf_op jit(solution)/shard_map/section/pallas_call | solution.py:341
  25.2 1.7 %copy.13 = f32[9,35,256]{2,1,0:T(8,128)} copy(f32[9,35,256]{2,1,0:T(8,128)} %section.1) | data formatting | bytes 645120

commit v2 on v1

--- a/solution.py
+++ b/solution.py
@@ -11,6 +11,7 @@
 NQ, NB, BP = 9, 35, 40
 FQ, FACES, E = 27, 4, 256
 ROWS, COLS, SLOTS = 32, 8, 64
+CHIPS = ROWS // 2
 LANES = 128
 WIDE = NQ * LANES
 KP = NQ * BP + 8
@@ -49,7 +50,7 @@
     normals, areas, out,
     st_v, mat_v, nb_v, sf_v, ve_v, vg_v, fe_v, fl_v, nrm_v, ar_v,
     recv, sendb, xr, sp, sb, raw, ohs, tr, pts, own, gath, flx, fx, vgm,
-    load_sem, gsend_sem, grecv_sem, tsend_sem, trecv_sem,
+    load_sem, gsend_sem, grecv_sem, tsend_sem, trecv_sem, ready_sem,
 ):
     row, col = lax.axis_index("row"), lax.axis_index("col")
     chip, core = row // 2, row % 2
@@ -71,17 +72,18 @@
 
     barrier = pltpu.get_barrier_semaphore()
 
-    @pl.loop(1, ROWS)
-    def _(d):
-        pl.semaphore_signal(
-            barrier, inc=1, device_id={"row": lax.rem(row + d, ROWS), "col": col}, device_id_type=MESH
-        )
+    def signal(sem, r, c):
+        pl.semaphore_signal(sem, inc=1, device_id={"row": r, "col": c}, device_id_type=MESH)
 
     @pl.loop(1, COLS)
     def _(d):
-        pl.semaphore_signal(
-            barrier, inc=1, device_id={"row": row, "col": lax.rem(col + d, COLS)}, device_id_type=MESH
-        )
+        signal(barrier, 2 * chip, lax.rem(col + d, COLS))
+
+    @pl.loop(1, CHIPS)
+    def _(d):
+        signal(barrier, 2 * lax.rem(chip + d, CHIPS) + 1, col)
+
+    signal(barrier, 2 * chip + (1 - core), col)
 
     def metric_copy(to, source):
         return pltpu.make_async_remote_copy(
@@ -142,19 +144,35 @@
         sendb[p] = outgoing[p * SLOTS : (p + 1) * SLOTS, :]
     xr[col] = jnp.zeros((SLOTS, 256), BF16)
 
-    pl.semaphore_wait(barrier, ROWS + COLS - 2)
+    @pl.when(core == 0)
+    def _():
+        pl.semaphore_wait(barrier, 2 * (COLS - 1) + 1)
+        signal(ready_sem, row + 1, col)
+
+    @pl.when(core == 1)
+    def _():
+        pl.semaphore_wait(ready_sem, 1)
+
+    @pl.loop(1, COLS)
+    def _(d):
+        trace_copy(lax.rem(col + d, COLS), col).start()
+
+    @pl.when(core == 1)
+    def _():
+        pl.semaphore_wait(barrier, ROWS - 1)
+        signal(ready_sem, row - 1, col)
+
+    @pl.when(core == 0)
+    def _():
+        pl.semaphore_wait(ready_sem, 1)
 
     metric_copy(2 * chip + (1 - core), row).start()
 
-    @pl.loop(1, 16)
+    @pl.loop(1, CHIPS)
     def _(o):
         peer = chip_at(o, 1)
         metric_copy(2 * peer + core, row).start()
         metric_copy(2 * peer + (1 - core), row).start()
-
-    @pl.loop(1, COLS)
-    def _(d):
-        trace_copy(lax.rem(col + d, COLS), col).start()
 
     for m in range(NQ):
         both = jnp.concatenate(
@@ -263,7 +281,7 @@
 
     surface = mm(lift, flx[...].reshape(8 * FQ, WIDE).astype(BF16))
 
-    @pl.loop(0, 16)
+    @pl.loop(0, CHIPS)
     def _(o):
         src = chip_at(o, -1)
         for a in range(2):
@@ -336,6 +354,7 @@
         state, geometry, material, neighbours, send_faces, vol_eval, vol_grad, face_eval, face_lift,
         normals, areas,
     )
+    args = tuple(pltpu.with_memory_space_constraint(a, pltpu.HBM) for a in args)
     staged = [a for i, a in enumerate(args) if i != 1]
     dma = pltpu.SemaphoreType.DMA
     return pl.pallas_call(
@@ -360,9 +379,10 @@
             pltpu.VMEM((3 * 256, WIDE), BF16),
             pltpu.VMEM((2 * BP, 3 * 256), BF16),
             dma((len(staged),)), dma((ROWS,)), dma((ROWS,)), dma((COLS,)), dma((COLS,)),
+            pltpu.SemaphoreType.REGULAR,
         ],
         compiler_params=pltpu.CompilerParams(
-            collective_id=0, has_side_effects=True, vmem_limit_bytes=60 * 1024 * 1024
+            collective_id=0, has_side_effects=True, vmem_limit_bytes=40 * 1024 * 1024
         ),
         name="section",
     )(*args)

time: 27 us -> 24.1 us (0.89)
  Pallas kernels: 25.1 us -> 23.3 us
  local copies, waits for them, and re-layouts: 1.75 us -> 0.74 us
    pallas_call x1, Pallas kernels: 25.1 us -> 23.3 us  [per_device(): pl.pallas_call(kernel, out_shape=jax.ShapeDtypeStruct((NQ, NB, E), F32),...]
    unnamed x1, local copies, waits for them, and re-layouts: 1.75 us -> 0.74 us
where the time goes in v2:
time: 24.1 us; the launch traced here: 24 us
  Pallas kernels  23.3 us (97%)
  local copies, waits for them, and re-layouts  0.74 us (3%)
    pallas_call x1, Pallas kernels, per_device(): pl.pallas_call(kernel, out_shape=jax.ShapeDtypeStruct((NQ, NB, E), F32),...  23.3 us
    unnamed x1, local copies, waits for them, and re-layouts  0.74 us

profile of v2, /device:TPU:1, one launch (start us, length us, event | category | flops | bytes accessed | tf_op | source)
XLA Modules:
  0.0 24.0 jit_solution(10247242401650324688)
XLA Ops:
  0.0 23.3 %section.1 = f32[9,35,256]{2,1,0:T(8,128)S(1)} custom-call(f32[9,35,256]{2,1,0:T(8,128)} %state.1, bf16[9,64,4,128]{3,2,1,0:T(4,128)(2,1)} %bitcast.5, f32[4,256]{1,0:T(4,128)} %material.1, s32[4,4,256]{2,1,0:T(4,128)} %neighbours.1, s32[1,8,64]{2,1,0:T(8,128)} %send_faces.1, f32[35,128]{1,0:T(8,128)} %vol_eval.1, bf16[3,35,128]{2,1,0:T(8,128)(2,1)} %vol_grad.1, ...), custom_call_target="tpu_custom_call" | custom-call | tf_op jit(solution)/shard_map/section/pallas_call | solution.py:360
  23.3 0.7 %copy.13 = f32[9,35,256]{2,1,0:T(8,128)} copy(f32[9,35,256]{2,1,0:T(8,128)S(1)} %section.1) | data formatting | bytes 645120

commit v3 on v2

--- a/solution.py
+++ b/solution.py
@@ -12,6 +12,8 @@
 FQ, FACES, E = 27, 4, 256
 ROWS, COLS, SLOTS = 32, 8, 64
 CHIPS = ROWS // 2
+EARLY = 4
+FAR = ((2, 2), (2, 1), (1, 2), (2, 3), (3, 2), (2, 0), (0, 2), (1, 1), (3, 3), (1, 3), (3, 1), (1, 0), (0, 1), (3, 0), (0, 3), (0, 0))
 LANES = 128
 WIDE = NQ * LANES
 KP = NQ * BP + 8
@@ -43,6 +45,14 @@
     for k in range(1, count):
         result = result + jnp.where(x >= size * k, 1, 0)
     return result
+
+
+def face_rows(source, raw):
+    raw[...] = jnp.zeros(raw.shape, F32)
+    for q in range(FQ):
+        for t in range(2):
+            raw[8 * q + 4 * t : 8 * q + 4 * t + 4, 0:NB] = source[q]
+    return raw[...].astype(BF16)
 
 
 def kernel(
@@ -101,8 +111,8 @@
         dx, dy = o // 4, o % 4
         return lax.rem(cx + sign * dx + 4, 4) * 4 + lax.rem(cy + sign * dy + 4, 4)
 
-    for copy in loads:
-        copy.wait()
+    for i in (0, 1, 3, 6):
+        loads[i].wait()
     for m in range(NQ):
         sp[m * BP : m * BP + NB, :] = st_v[m]
         sp[m * BP + NB : (m + 1) * BP, :] = jnp.zeros((BP - NB, E), F32)
@@ -112,13 +122,7 @@
     sp[NQ * BP + 6 : KP, :] = jnp.zeros((2, E), F32)
     dof = sp[...].astype(BF16)
 
-    raw[...] = jnp.zeros(raw.shape, F32)
-    for q in range(FQ):
-        for t in range(2):
-            raw[0, 8 * q + 4 * t : 8 * q + 4 * t + 4, 0:NB] = fe_v[q]
-            raw[1, 8 * q + 4 * t : 8 * q + 4 * t + 4, 0:NB] = fl_v[q]
-    eval_rows = raw[0].astype(BF16)
-    lift_rows = raw[1].astype(BF16)
+    eval_rows = face_rows(fe_v, raw.at[0])
 
     col_kp = iota((1, KP), 1)
     m_col = steps(col_kp, BP, NQ)
@@ -144,35 +148,54 @@
         sendb[p] = outgoing[p * SLOTS : (p + 1) * SLOTS, :]
     xr[col] = jnp.zeros((SLOTS, 256), BF16)
 
-    @pl.when(core == 0)
+    def wait_column():
+        @pl.when(core == 0)
+        def _():
+            pl.semaphore_wait(barrier, 2 * (COLS - 1) + 1)
+            signal(ready_sem, row + 1, col)
+
+        @pl.when(core == 1)
+        def _():
+            pl.semaphore_wait(ready_sem, 1)
+
+    def wait_plane():
+        @pl.when(core == 1)
+        def _():
+            pl.semaphore_wait(barrier, ROWS - 1)
+            signal(ready_sem, row - 1, col)
+
+        @pl.when(core == 0)
+        def _():
+            pl.semaphore_wait(ready_sem, 1)
+
+    def send_traces():
+        @pl.loop(0, COLS - 1)
+        def _(i):
+            trace_copy(i + jnp.where(i >= col, 1, 0), col).start()
+
+    def send_metric():
+        for dx, dy in FAR:
+            peer = lax.rem(cx + dx, 4) * 4 + lax.rem(cy + dy, 4)
+            if (dx, dy) != (0, 0):
+                metric_copy(2 * peer + core, row).start()
+            metric_copy(2 * peer + (1 - core), row).start()
+
+    @pl.when(col >= EARLY)
     def _():
-        pl.semaphore_wait(barrier, 2 * (COLS - 1) + 1)
-        signal(ready_sem, row + 1, col)
-
-    @pl.when(core == 1)
+        wait_column()
+        send_traces()
+        wait_plane()
+        send_metric()
+
+    @pl.when(col < EARLY)
     def _():
-        pl.semaphore_wait(ready_sem, 1)
-
-    @pl.loop(1, COLS)
-    def _(d):
-        trace_copy(lax.rem(col + d, COLS), col).start()
-
-    @pl.when(core == 1)
-    def _():
-        pl.semaphore_wait(barrier, ROWS - 1)
-        signal(ready_sem, row - 1, col)
-
-    @pl.when(core == 0)
-    def _():
-        pl.semaphore_wait(ready_sem, 1)
-
-    metric_copy(2 * chip + (1 - core), row).start()
-
-    @pl.loop(1, CHIPS)
-    def _(o):
-        peer = chip_at(o, 1)
-        metric_copy(2 * peer + core, row).start()
-        metric_copy(2 * peer + (1 - core), row).start()
+        wait_plane()
+        send_metric()
+        wait_column()
+        send_traces()
+
+    for i in (2, 4, 5, 7, 8, 9):
+        loads[i].wait()
 
     for m in range(NQ):
         both = jnp.concatenate(
@@ -200,6 +223,7 @@
         vgm[:, d * 256 : (d + 1) * 256] = jnp.where(grad_mask, mm_t(grad2, spread_v), 0.0).astype(BF16)
     twice_t = ones_where(iota((2 * BP, 1), 0) - BP * tile_row == iota((1, BP), 1))
     lift_mask = tile_row == ((iota((1, 8 * FQ), 1) >> 2) & 1)
+    lift_rows = face_rows(fl_v, raw.at[1])
     lift = jnp.where(lift_mask, mm_t(twice_t, lift_rows), 0.0).astype(BF16)
 
     kind, peer, target, turn = nb_v[0], nb_v[1], nb_v[2], nb_v[3]

time: 24.1 us -> 19.7 us (0.82)
  Pallas kernels: 23.3 us -> 18.9 us
    pallas_call x1, Pallas kernels: 23.3 us -> 18.9 us  [per_device(): pl.pallas_call(kernel, out_shape=jax.ShapeDtypeStruct((NQ, NB, E), F32),...]
where the time goes in v3:
time: 19.7 us; the launch traced here: 19.6 us
  Pallas kernels  18.9 us (96%)
  local copies, waits for them, and re-layouts  0.74 us (4%)
    pallas_call x1, Pallas kernels, per_device(): pl.pallas_call(kernel, out_shape=jax.ShapeDtypeStruct((NQ, NB, E), F32),...  18.9 us
    unnamed x1, local copies, waits for them, and re-layouts  0.74 us

profile of v3, /device:TPU:1, one launch (start us, length us, event | category | flops | bytes accessed | tf_op | source)
XLA Modules:
  0.0 19.6 jit_solution(18157186780906961286)
XLA Ops:
  0.0 18.9 %section.1 = f32[9,35,256]{2,1,0:T(8,128)S(1)} custom-call(f32[9,35,256]{2,1,0:T(8,128)} %state.1, bf16[9,64,4,128]{3,2,1,0:T(4,128)(2,1)} %bitcast.5, f32[4,256]{1,0:T(4,128)} %material.1, s32[4,4,256]{2,1,0:T(4,128)} %neighbours.1, s32[1,8,64]{2,1,0:T(8,128)} %send_faces.1, f32[35,128]{1,0:T(8,128)} %vol_eval.1, bf16[3,35,128]{2,1,0:T(8,128)(2,1)} %vol_grad.1, ...), custom_call_target="tpu_custom_call" | custom-call | tf_op jit(solution)/shard_map/section/pallas_call | solution.py:384
  18.9 0.7 %copy.13 = f32[9,35,256]{2,1,0:T(8,128)} copy(f32[9,35,256]{2,1,0:T(8,128)S(1)} %section.1) | data formatting | bytes 645120

commit v4 on v3

--- a/solution.py
+++ b/solution.py
@@ -18,6 +18,7 @@
 WIDE = NQ * LANES
 KP = NQ * BP + 8
 PITCH = 264
+ORDER = FAR[-1:] + FAR[:-1]
 
 
 def iota(shape, dim):
@@ -59,12 +60,28 @@
     state, geometry, material, neighbours, send_faces, vol_eval, vol_grad, face_eval, face_lift,
     normals, areas, out,
     st_v, mat_v, nb_v, sf_v, ve_v, vg_v, fe_v, fl_v, nrm_v, ar_v,
-    recv, sendb, xr, sp, sb, raw, ohs, tr, pts, own, gath, flx, fx, vgm,
+    recv, sendb, xr, sp, sb, raw, ohs, ohr, tr, pts, own, gath, flx, fx, vgm,
     load_sem, gsend_sem, grecv_sem, tsend_sem, trecv_sem, ready_sem,
 ):
     row, col = lax.axis_index("row"), lax.axis_index("col")
     chip, core = row // 2, row % 2
     cx, cy = chip // 4, chip % 4
+
+    def neighbour(dx, dy):
+        return ((cx + dx) & 3) * 4 + ((cy + dy) & 3)
+
+    barrier = pltpu.get_barrier_semaphore()
+
+    def signal(sem, r, c):
+        pl.semaphore_signal(sem, inc=1, device_id={"row": r, "col": c}, device_id_type=MESH)
+
+    for d in (4, 3, 5, 2, 6, 1, 7):
+        signal(barrier, 2 * chip, lax.rem(col + d, COLS))
+
+    for dx, dy in FAR[:-1]:
+        signal(barrier, 2 * neighbour(dx, dy) + 1, col)
+
+    signal(barrier, 2 * chip + (1 - core), col)
 
     pairs = [
         (state, st_v), (material, mat_v), (neighbours, nb_v), (send_faces, sf_v), (vol_eval, ve_v),
@@ -80,36 +97,17 @@
     local = pltpu.make_async_copy(block(row), recv.at[row], grecv_sem.at[row])
     local.start()
 
-    barrier = pltpu.get_barrier_semaphore()
-
-    def signal(sem, r, c):
-        pl.semaphore_signal(sem, inc=1, device_id={"row": r, "col": c}, device_id_type=MESH)
-
-    @pl.loop(1, COLS)
-    def _(d):
-        signal(barrier, 2 * chip, lax.rem(col + d, COLS))
-
-    @pl.loop(1, CHIPS)
-    def _(d):
-        signal(barrier, 2 * lax.rem(chip + d, CHIPS) + 1, col)
-
-    signal(barrier, 2 * chip + (1 - core), col)
-
     def metric_copy(to, source):
         return pltpu.make_async_remote_copy(
-            src_ref=block(to), dst_ref=recv.at[source], send_sem=gsend_sem.at[to],
+            src_ref=block(to), dst_ref=recv.at[source], send_sem=gsend_sem,
             recv_sem=grecv_sem.at[source], device_id={"row": to, "col": col}, device_id_type=MESH,
         )
 
     def trace_copy(to, source):
         return pltpu.make_async_remote_copy(
-            src_ref=sendb.at[to], dst_ref=xr.at[source], send_sem=tsend_sem.at[to],
-            recv_sem=trecv_sem.at[source], device_id={"row": row, "col": to}, device_id_type=MESH,
-        )
-
-    def chip_at(o, sign):
-        dx, dy = o // 4, o % 4
-        return lax.rem(cx + sign * dx + 4, 4) * 4 + lax.rem(cy + sign * dy + 4, 4)
+            src_ref=sendb.at[to], dst_ref=xr.at[source], send_sem=tsend_sem,
+            recv_sem=trecv_sem, device_id={"row": row, "col": to}, device_id_type=MESH,
+        )
 
     for i in (0, 1, 3, 6):
         loads[i].wait()
@@ -175,7 +173,7 @@
 
     def send_metric():
         for dx, dy in FAR:
-            peer = lax.rem(cx + dx, 4) * 4 + lax.rem(cy + dy, 4)
+            peer = neighbour(dx, dy)
             if (dx, dy) != (0, 0):
                 metric_copy(2 * peer + core, row).start()
             metric_copy(2 * peer + (1 - core), row).start()
@@ -236,15 +234,61 @@
         for t in range(2):
             gath[(4 * t + f) * PITCH : (4 * t + f) * PITCH + 256, :] = got[:, t * LANES : (t + 1) * LANES]
 
-    @pl.loop(1, COLS)
-    def _(d):
-        source = lax.rem(col + COLS - d, COLS)
-        trace_copy(source, source).wait_recv()
-
+        ohr[:, f * E : (f + 1) * E] = ones_where(
+            iota((COLS * SLOTS, 1), 0) + FACES * E == code[f : f + 1, :]
+        )
     ident = ones_where(iota((256, 1), 0) == iota((1, 256), 1))
+    def all_metric():
+        part = recv.at[pl.ds(0, ROWS - 1)]
+        return pltpu.make_async_remote_copy(
+            src_ref=part, dst_ref=part, send_sem=gsend_sem, recv_sem=grecv_sem.at[0],
+            device_id={"row": lax.rem(row + 1, ROWS), "col": col}, device_id_type=MESH,
+        )
+
+    def chip_products(dx, dy):
+        src = neighbour(-dx, -dy)
+        for a in range(2):
+            metric_copy(2 * src + a, 2 * src + a).wait_recv()
+        at = pl.multiple_of(16 * src, 16)
+        u = [pts[pl.ds(at, 16), m * LANES : (m + 1) * LANES] for m in range(NQ)]
+        for d in range(3):
+            n = [
+                jnp.concatenate(
+                    [got8(recv, 2 * src, 3 * d + j), got8(recv, 2 * src + 1, 3 * d + j)], axis=0
+                )
+                for j in range(3)
+            ]
+            product = [
+                n[0] * u[6],
+                n[1] * u[7],
+                n[2] * u[8],
+                n[0] * u[7] + n[1] * u[6],
+                n[1] * u[8] + n[2] * u[7],
+                n[0] * u[8] + n[2] * u[6],
+                u[0] * n[0] + u[3] * n[1] + u[5] * n[2],
+                u[3] * n[0] + u[1] * n[1] + u[4] * n[2],
+                u[5] * n[0] + u[4] * n[1] + u[2] * n[2],
+            ]
+            for m in range(NQ):
+                fx[pl.ds(pl.multiple_of(d * 256 + at, 16), 16), m * LANES : (m + 1) * LANES] = product[
+                    m
+                ].astype(BF16)
+
+    for dx, dy in ORDER[:12]:
+        chip_products(dx, dy)
+
+    def all_traces():
+        part = xr.at[pl.ds(0, COLS - 1)]
+        return pltpu.make_async_remote_copy(
+            src_ref=part, dst_ref=part, send_sem=tsend_sem, recv_sem=trecv_sem,
+            device_id={"row": row, "col": lax.rem(col + 1, COLS)}, device_id_type=MESH,
+        )
+
+    all_traces().wait_recv()
+
     xt = mm_t(ident, xr[...].reshape(COLS * SLOTS, 256)).astype(BF16)
     for f in range(FACES):
-        got = mm(xt, ones_where(iota((COLS * SLOTS, 1), 0) + FACES * E == code[f : f + 1, :]))
+        got = mm(xt, ohr[:, f * E : (f + 1) * E])
         for t in range(2):
             at = (4 * t + f) * PITCH
             gath[at : at + 256, :] = gath[at : at + 256, :] + got[:, t * LANES : (t + 1) * LANES]
@@ -305,36 +349,11 @@
 
     surface = mm(lift, flx[...].reshape(8 * FQ, WIDE).astype(BF16))
 
-    @pl.loop(0, CHIPS)
-    def _(o):
-        src = chip_at(o, -1)
-        for a in range(2):
-            metric_copy(2 * src + a, 2 * src + a).wait_recv()
-        at = pl.multiple_of(16 * src, 16)
-        u = [pts[pl.ds(at, 16), m * LANES : (m + 1) * LANES] for m in range(NQ)]
-        for d in range(3):
-            n = [
-                jnp.concatenate(
-                    [got8(recv, 2 * src, 3 * d + j), got8(recv, 2 * src + 1, 3 * d + j)], axis=0
-                )
-                for j in range(3)
-            ]
-            product = [
-                n[0] * u[6],
-                n[1] * u[7],
-                n[2] * u[8],
-                n[0] * u[7] + n[1] * u[6],
-                n[1] * u[8] + n[2] * u[7],
-                n[0] * u[8] + n[2] * u[6],
-                u[0] * n[0] + u[3] * n[1] + u[5] * n[2],
-                u[3] * n[0] + u[1] * n[1] + u[4] * n[2],
-                u[5] * n[0] + u[4] * n[1] + u[2] * n[2],
-            ]
-            for m in range(NQ):
-                fx[pl.ds(pl.multiple_of(d * 256 + at, 16), 16), m * LANES : (m + 1) * LANES] = product[
-                    m
-                ].astype(BF16)
-
+    for dx, dy in ORDER[12:]:
+        chip_products(dx, dy)
+
+    all_metric().wait_send()
+    all_traces().wait_send()
     volume = mm(vgm[...], fx[...])
     for t in range(2):
         rows = slice(t * BP, (t + 1) * BP)
@@ -351,16 +370,6 @@
                 total = -w * v[m]
             total = total - surface[rows, m * LANES : (m + 1) * LANES]
             out[m, :, lanes] = st_v[m, :, lanes] + (step * total)[0:NB]
-
-    @pl.loop(1, ROWS)
-    def _(d):
-        to = lax.rem(row + d, ROWS)
-        metric_copy(to, row).wait_send()
-
-    @pl.loop(1, COLS)
-    def _(d):
-        to = lax.rem(col + d, COLS)
-        trace_copy(to, col).wait_send()
 
 
 def got8(recv, r, k):
@@ -395,6 +404,7 @@
             pltpu.VMEM((2 * BP, WIDE), BF16),
             pltpu.VMEM((2, 8 * FQ, BP), F32),
             pltpu.VMEM((COLS * SLOTS, FACES * E), BF16),
+            pltpu.VMEM((COLS * SLOTS, FACES * E), BF16),
             pltpu.VMEM((256, FACES * E), BF16),
             pltpu.VMEM((256, WIDE), F32),
             pltpu.VMEM((FQ, 8, WIDE), F32),
@@ -402,7 +412,7 @@
             pltpu.VMEM((FQ, 8, WIDE), F32),
             pltpu.VMEM((3 * 256, WIDE), BF16),
             pltpu.VMEM((2 * BP, 3 * 256), BF16),
-            dma((len(staged),)), dma((ROWS,)), dma((ROWS,)), dma((COLS,)), dma((COLS,)),
+            dma((len(staged),)), pltpu.SemaphoreType.DMA, dma((ROWS,)), pltpu.SemaphoreType.DMA, pltpu.SemaphoreType.DMA,
             pltpu.SemaphoreType.REGULAR,
         ],
         compiler_params=pltpu.CompilerParams(

time: 19.7 us -> 18.3 us (0.929)
  Pallas kernels: 18.9 us -> 17.4 us
    pallas_call x1, Pallas kernels: 18.9 us -> 17.4 us  [per_device(): pl.pallas_call(kernel, out_shape=jax.ShapeDtypeStruct((NQ, NB, E), F32),...]
where the time goes in v4:
time: 18.3 us; the launch traced here: 18.2 us
  Pallas kernels  17.4 us (95%)
  local copies, waits for them, and re-layouts  0.74 us (4%)
    pallas_call x1, Pallas kernels, per_device(): pl.pallas_call(kernel, out_shape=jax.ShapeDtypeStruct((NQ, NB, E), F32),...  17.4 us
    unnamed x1, local copies, waits for them, and re-layouts  0.74 us

profile of v4, /device:TPU:1, one launch (start us, length us, event | category | flops | bytes accessed | tf_op | source)
XLA Modules:
  0.0 18.2 jit_solution(8806462155889414954)
XLA Ops:
  0.0 17.4 %section.1 = f32[9,35,256]{2,1,0:T(8,128)S(1)} custom-call(f32[9,35,256]{2,1,0:T(8,128)} %state.1, bf16[9,64,4,128]{3,2,1,0:T(4,128)(2,1)} %bitcast.5, f32[4,256]{1,0:T(4,128)} %material.1, s32[4,4,256]{2,1,0:T(4,128)} %neighbours.1, s32[1,8,64]{2,1,0:T(8,128)} %send_faces.1, f32[35,128]{1,0:T(8,128)} %vol_eval.1, bf16[3,35,128]{2,1,0:T(8,128)(2,1)} %vol_grad.1, ...), custom_call_target="tpu_custom_call" | custom-call | tf_op jit(solution)/shard_map/section/pallas_call | solution.py:393
  17.4 0.7 %copy.13 = f32[9,35,256]{2,1,0:T(8,128)} copy(f32[9,35,256]{2,1,0:T(8,128)S(1)} %section.1) | data formatting | bytes 645120

commit v5 on v4

--- a/solution.py
+++ b/solution.py
@@ -59,7 +59,7 @@
 def kernel(
     state, geometry, material, neighbours, send_faces, vol_eval, vol_grad, face_eval, face_lift,
     normals, areas, out,
-    st_v, mat_v, nb_v, sf_v, ve_v, vg_v, fe_v, fl_v, nrm_v, ar_v,
+    geo_v, st_v, mat_v, nb_v, sf_v, ve_v, vg_v, fe_v, fl_v, nrm_v, ar_v,
     recv, sendb, xr, sp, sb, raw, ohs, ohr, tr, pts, own, gath, flx, fx, vgm,
     load_sem, gsend_sem, grecv_sem, tsend_sem, trecv_sem, ready_sem,
 ):
@@ -91,11 +91,16 @@
     for copy in loads:
         copy.start()
 
+    stage = pltpu.make_async_copy(geometry, geo_v, load_sem.at[len(pairs)])
+    stage.start()
+    local = pltpu.make_async_copy(
+        geometry.at[:, pl.ds(2 * row, 2)], recv.at[row], grecv_sem.at[row]
+    )
+    local.start()
+
     def block(p):
-        return geometry.at[:, pl.ds(2 * p, 2)]
-
-    local = pltpu.make_async_copy(block(row), recv.at[row], grecv_sem.at[row])
-    local.start()
+        return geo_v.at[:, pl.ds(2 * p, 2)]
+
 
     def metric_copy(to, source):
         return pltpu.make_async_remote_copy(
@@ -172,6 +177,7 @@
             trace_copy(i + jnp.where(i >= col, 1, 0), col).start()
 
     def send_metric():
+        stage.wait()
         for dx, dy in FAR:
             peer = neighbour(dx, dy)
             if (dx, dy) != (0, 0):
@@ -395,7 +401,7 @@
         out_shape=jax.ShapeDtypeStruct((NQ, NB, E), F32),
         in_specs=[pl.BlockSpec(memory_space=pl.ANY)] * len(args),
         out_specs=pl.BlockSpec(memory_space=pltpu.VMEM),
-        scratch_shapes=[pltpu.VMEM(a.shape, a.dtype) for a in staged]
+        scratch_shapes=[pltpu.VMEM(a.shape, a.dtype) for a in (args[1], *staged)]
         + [
             pltpu.VMEM((ROWS, 9, 2, 4, LANES), BF16),
             pltpu.VMEM((COLS, SLOTS, 256), BF16),
@@ -412,7 +418,7 @@
             pltpu.VMEM((FQ, 8, WIDE), F32),
             pltpu.VMEM((3 * 256, WIDE), BF16),
             pltpu.VMEM((2 * BP, 3 * 256), BF16),
-            dma((len(staged),)), pltpu.SemaphoreType.DMA, dma((ROWS,)), pltpu.SemaphoreType.DMA, pltpu.SemaphoreType.DMA,
+            dma((len(args),)), pltpu.SemaphoreType.DMA, dma((ROWS,)), pltpu.SemaphoreType.DMA, pltpu.SemaphoreType.DMA,
             pltpu.SemaphoreType.REGULAR,
         ],
         compiler_params=pltpu.CompilerParams(

time: 18.3 us -> 18.1 us (0.989)
  Pallas kernels: 17.4 us -> 17.2 us
    pallas_call x1, Pallas kernels: 17.4 us -> 17.2 us  [per_device(): pl.pallas_call(kernel, out_shape=jax.ShapeDtypeStruct((NQ, NB, E), F32),...]
where the time goes in v5:
time: 18.1 us; the launch traced here: 18 us
  Pallas kernels  17.2 us (95%)
  local copies, waits for them, and re-layouts  0.74 us (4%)
    pallas_call x1, Pallas kernels, per_device(): pl.pallas_call(kernel, out_shape=jax.ShapeDtypeStruct((NQ, NB, E), F32),...  17.2 us
    unnamed x1, local copies, waits for them, and re-layouts  0.74 us

profile of v5, /device:TPU:1, one launch (start us, length us, event | category | flops | bytes accessed | tf_op | source)
XLA Modules:
  0.0 18.0 jit_solution(10467886192451177329)
XLA Ops:
  0.0 17.2 %section.1 = f32[9,35,256]{2,1,0:T(8,128)S(1)} custom-call(f32[9,35,256]{2,1,0:T(8,128)} %state.1, bf16[9,64,4,128]{3,2,1,0:T(4,128)(2,1)} %bitcast.5, f32[4,256]{1,0:T(4,128)} %material.1, s32[4,4,256]{2,1,0:T(4,128)} %neighbours.1, s32[1,8,64]{2,1,0:T(8,128)} %send_faces.1, f32[35,128]{1,0:T(8,128)} %vol_eval.1, bf16[3,35,128]{2,1,0:T(8,128)(2,1)} %vol_grad.1, ...), custom_call_target="tpu_custom_call" | custom-call | tf_op jit(solution)/shard_map/section/pallas_call | solution.py:399
  17.2 0.7 %copy.13 = f32[9,35,256]{2,1,0:T(8,128)} copy(f32[9,35,256]{2,1,0:T(8,128)S(1)} %section.1) | data formatting | bytes 645120

commit v6 on v5

--- a/solution.py
+++ b/solution.py
@@ -19,6 +19,7 @@
 KP = NQ * BP + 8
 PITCH = 264
 ORDER = FAR[-1:] + FAR[:-1]
+FIRST, LAST = ORDER[:12], ORDER[12:]
 
 
 def iota(shape, dim):
@@ -56,41 +57,60 @@
     return raw[...].astype(BF16)
 
 
+def face_flux(u, lame, rigid, buoyancy, n):
+    r = [rigid * u[6 + j] for j in range(3)]
+    s = [buoyancy * u[i] for i in range(6)]
+    pressure = lame * (n[0] * u[6] + n[1] * u[7] + n[2] * u[8])
+    return [
+        pressure + 2.0 * (n[0] * r[0]),
+        pressure + 2.0 * (n[1] * r[1]),
+        pressure + 2.0 * (n[2] * r[2]),
+        n[0] * r[1] + n[1] * r[0],
+        n[1] * r[2] + n[2] * r[1],
+        n[0] * r[2] + n[2] * r[0],
+        s[0] * n[0] + s[3] * n[1] + s[5] * n[2],
+        s[3] * n[0] + s[1] * n[1] + s[4] * n[2],
+        s[5] * n[0] + s[4] * n[1] + s[2] * n[2],
+    ]
+
+
 def kernel(
     state, geometry, material, neighbours, send_faces, vol_eval, vol_grad, face_eval, face_lift,
     normals, areas, out,
     geo_v, st_v, mat_v, nb_v, sf_v, ve_v, vg_v, fe_v, fl_v, nrm_v, ar_v,
-    recv, sendb, xr, sp, sb, raw, ohs, ohr, tr, pts, own, gath, flx, fx, vgm,
+    recv, sendb, xr, sp, sb, raw, ohs, ohr, tr, pts, own, gath, flx, fx_a, fx_b, vg_a, vg_b, acc, base, geo8,
     load_sem, gsend_sem, grecv_sem, tsend_sem, trecv_sem, ready_sem,
 ):
     row, col = lax.axis_index("row"), lax.axis_index("col")
     chip, core = row // 2, row % 2
     cx, cy = chip // 4, chip % 4
 
-    def neighbour(dx, dy):
-        return ((cx + dx) & 3) * 4 + ((cy + dy) & 3)
-
-    barrier = pltpu.get_barrier_semaphore()
-
-    def signal(sem, r, c):
-        pl.semaphore_signal(sem, inc=1, device_id={"row": r, "col": c}, device_id_type=MESH)
-
-    for d in (4, 3, 5, 2, 6, 1, 7):
-        signal(barrier, 2 * chip, lax.rem(col + d, COLS))
-
-    for dx, dy in FAR[:-1]:
-        signal(barrier, 2 * neighbour(dx, dy) + 1, col)
-
-    signal(barrier, 2 * chip + (1 - core), col)
-
     pairs = [
         (state, st_v), (material, mat_v), (neighbours, nb_v), (send_faces, sf_v), (vol_eval, ve_v),
         (vol_grad, vg_v), (face_eval, fe_v), (face_lift, fl_v), (normals, nrm_v), (areas, ar_v),
     ]
     loads = [pltpu.make_async_copy(a, b, load_sem.at[i]) for i, (a, b) in enumerate(pairs)]
-    for copy in loads:
-        copy.start()
-
+    for i in (0, 6, 3, 1):
+        loads[i].start()
+
+    def neighbour(dx, dy):
+        return ((cx + dx) & 3) * 4 + ((cy + dy) & 3)
+
+    barrier = pltpu.get_barrier_semaphore()
+
+    def signal(sem, r, c):
+        pl.semaphore_signal(sem, inc=1, device_id={"row": r, "col": c}, device_id_type=MESH)
+
+    for d in (4, 3, 5, 2, 6, 1, 7):
+        signal(barrier, 2 * chip, lax.rem(col + d, COLS))
+
+    for dx, dy in FAR[:-1]:
+        signal(barrier, 2 * neighbour(dx, dy) + 1, col)
+
+    signal(barrier, 2 * chip + (1 - core), col)
+
+    for i in (2, 4, 5, 7, 8, 9):
+        loads[i].start()
     stage = pltpu.make_async_copy(geometry, geo_v, load_sem.at[len(pairs)])
     stage.start()
     local = pltpu.make_async_copy(
@@ -178,11 +198,21 @@
 
     def send_metric():
         stage.wait()
-        for dx, dy in FAR:
+        far = (chip != 0) & (col == 0)
+
+        @pl.when(far)
+        def _():
+            metric_copy(1, row).start()
+
+        for dx, dy in FAR[:-1]:
             peer = neighbour(dx, dy)
-            if (dx, dy) != (0, 0):
-                metric_copy(2 * peer + core, row).start()
-            metric_copy(2 * peer + (1 - core), row).start()
+
+            @pl.when(jnp.logical_not(far & (peer == 0)))
+            def _(peer=peer):
+                metric_copy(2 * peer + 1, row).start()
+
+            metric_copy(2 * peer, row).start()
+        metric_copy(2 * chip + (1 - core), row).start()
 
     @pl.when(col >= EARLY)
     def _():
@@ -220,11 +250,23 @@
     vol_weights = jnp.where(vol_mask, mm_t(spread_v, eval2), 0.0).astype(BF16)
     pts[...] = mm(vol_weights, sb[...])
     tile_row = jnp.where(iota((2 * BP, 1), 0) >= BP, 1, 0)
-    grad_mask = tile_row == ((iota((1, 256), 1) >> 2) & 1)
+    grads = []
     for d in range(3):
         grad = vg_v[d].astype(F32)
-        grad2 = jnp.concatenate([grad, pad, grad, pad], axis=0).astype(BF16)
-        vgm[:, d * 256 : (d + 1) * 256] = jnp.where(grad_mask, mm_t(grad2, spread_v), 0.0).astype(BF16)
+        grads.append(jnp.concatenate([grad, pad, grad, pad], axis=0).astype(BF16))
+    for part, weights in ((FIRST, vg_a), (LAST, vg_b)):
+        size = 16 * len(part)
+        at_row = iota((size, 1), 0)
+        source = jnp.zeros((size, 1), I32)
+        for i, (dx, dy) in enumerate(part):
+            source = jnp.where((at_row >> 4) == i, neighbour(-dx, -dy), source)
+        point = 8 * source + 4 * ((at_row >> 3) & 1) + (at_row & 3)
+        spread = ones_where(iota((1, 128), 1) == point)
+        grad_mask = tile_row == ((iota((1, size), 1) >> 2) & 1)
+        for d in range(3):
+            weights[:, d * size : (d + 1) * size] = jnp.where(
+                grad_mask, mm_t(grads[d], spread), 0.0
+            ).astype(BF16)
     twice_t = ones_where(iota((2 * BP, 1), 0) - BP * tile_row == iota((1, BP), 1))
     lift_mask = tile_row == ((iota((1, 8 * FQ), 1) >> 2) & 1)
     lift_rows = face_rows(fl_v, raw.at[1])
@@ -244,6 +286,30 @@
             iota((COLS * SLOTS, 1), 0) + FACES * E == code[f : f + 1, :]
         )
     ident = ones_where(iota((256, 1), 0) == iota((1, 256), 1))
+    def gathered(r):
+        return gath[pl.ds(r, 8, stride=PITCH), :]
+
+    def per_face(i):
+        return jnp.concatenate(
+            [jnp.broadcast_to(mat_v[i : i + 1, t * LANES : (t + 1) * LANES], (4, LANES)) for t in range(2)],
+            axis=0,
+        )
+
+    kind8, turn8 = halves(kind), halves(turn)
+    l1, g1, w1 = per_face(0), per_face(1), per_face(2)
+    speed = jnp.sqrt((l1 + 2.0 * g1) * w1)
+    l1, g1, w1 = 0.5 * l1, 0.5 * g1, 0.5 * w1
+
+    @pl.loop(0, FQ)
+    def _(q):
+        n = [halves(nrm_v[j, q].astype(F32)) for j in range(3)]
+        for j in range(3):
+            geo8[q, :, j * LANES : (j + 1) * LANES] = n[j]
+        geo8[q, :, 3 * LANES : 4 * LANES] = halves(ar_v[q])
+        flux = face_flux([own[q, :, m * LANES : (m + 1) * LANES] for m in range(NQ)], l1, g1, w1, n)
+        for m in range(NQ):
+            base[q, :, m * LANES : (m + 1) * LANES] = -flux[m]
+
     def all_metric():
         part = recv.at[pl.ds(0, ROWS - 1)]
         return pltpu.make_async_remote_copy(
@@ -251,7 +317,7 @@
             device_id={"row": lax.rem(row + 1, ROWS), "col": col}, device_id_type=MESH,
         )
 
-    def chip_products(dx, dy):
+    def chip_products(dx, dy, i, size, fx):
         src = neighbour(-dx, -dy)
         for a in range(2):
             metric_copy(2 * src + a, 2 * src + a).wait_recv()
@@ -276,12 +342,13 @@
                 u[5] * n[0] + u[4] * n[1] + u[2] * n[2],
             ]
             for m in range(NQ):
-                fx[pl.ds(pl.multiple_of(d * 256 + at, 16), 16), m * LANES : (m + 1) * LANES] = product[
+                fx[d * size + 16 * i : d * size + 16 * i + 16, m * LANES : (m + 1) * LANES] = product[
                     m
                 ].astype(BF16)
 
-    for dx, dy in ORDER[:12]:
-        chip_products(dx, dy)
+    for i, (dx, dy) in enumerate(FIRST):
+        chip_products(dx, dy, i, 16 * len(FIRST), fx_a)
+    acc[...] = mm(vg_a[...], fx_a[...])
 
     def all_traces():
         part = xr.at[pl.ds(0, COLS - 1)]
@@ -299,23 +366,11 @@
             at = (4 * t + f) * PITCH
             gath[at : at + 256, :] = gath[at : at + 256, :] + got[:, t * LANES : (t + 1) * LANES]
 
-    def gathered(r):
-        return gath[pl.ds(r, 8, stride=PITCH), :]
-
-    def per_face(i):
-        return jnp.concatenate(
-            [jnp.broadcast_to(mat_v[i : i + 1, t * LANES : (t + 1) * LANES], (4, LANES)) for t in range(2)],
-            axis=0,
-        )
-
-    kind8, turn8 = halves(kind), halves(turn)
-    l1, g1, w1 = per_face(0), per_face(1), per_face(2)
     l2, g2, w2 = [gathered(NQ * FQ + i) + gathered(NQ * FQ + 3 + i) for i in range(3)]
-    fastest = 0.5 * jnp.maximum(jnp.sqrt((l1 + 2.0 * g1) * w1), jnp.sqrt((l2 + 2.0 * g2) * w2))
+    fastest = 0.5 * jnp.maximum(speed, jnp.sqrt((l2 + 2.0 * g2) * w2))
     sign_v = jnp.where(kind8 == 3, 0.0, 1.0)
     sign_s = jnp.where(kind8 == 2, -1.0, sign_v)
-    l1, g1, w1 = 0.5 * l1, 0.5 * g1, 0.5 * w1
-    l2, g2, w2 = 0.5 * l2 * sign_v, 0.5 * g2 * sign_v, 0.5 * w2 * sign_s
+    l2, g2, w2 = 0.5 * l2, 0.5 * g2, 0.5 * w2
     turn_one, turn_two = turn8 == 1, turn8 == 2
 
     @pl.loop(0, FQ // 3)
@@ -324,43 +379,29 @@
         outer = [[], [], []]
         for m in range(NQ):
             g = [gathered(m * FQ + q0 + k) for k in range(3)]
+            sign = sign_s if m < 6 else sign_v
             for k in range(3):
                 outer[k].append(
-                    jnp.where(turn_one, g[(k + 1) % 3], jnp.where(turn_two, g[(k + 2) % 3], g[k]))
+                    sign
+                    * jnp.where(turn_one, g[(k + 1) % 3], jnp.where(turn_two, g[(k + 2) % 3], g[k]))
                 )
         for k in range(3):
             q = q0 + k
-            o = outer[k]
-            u = [own[q, :, m * LANES : (m + 1) * LANES] for m in range(NQ)]
-            n = [halves(nrm_v[j, q].astype(F32)) for j in range(3)]
-            penalty = fastest * halves(ar_v[q])
-            rigid = [g1 * u[6 + j] + g2 * o[6 + j] for j in range(3)]
-            lame = [l1 * u[6 + j] + l2 * o[6 + j] for j in range(3)]
-            stress = [w1 * u[s] + w2 * o[s] for s in range(6)]
-            pressure = n[0] * lame[0] + n[1] * lame[1] + n[2] * lame[2]
-            flux = [
-                pressure + 2.0 * (n[0] * rigid[0]),
-                pressure + 2.0 * (n[1] * rigid[1]),
-                pressure + 2.0 * (n[2] * rigid[2]),
-                n[0] * rigid[1] + n[1] * rigid[0],
-                n[1] * rigid[2] + n[2] * rigid[1],
-                n[0] * rigid[2] + n[2] * rigid[0],
-                stress[0] * n[0] + stress[3] * n[1] + stress[5] * n[2],
-                stress[3] * n[0] + stress[1] * n[1] + stress[4] * n[2],
-                stress[5] * n[0] + stress[4] * n[1] + stress[2] * n[2],
-            ]
+            n = [geo8[q, :, j * LANES : (j + 1) * LANES] for j in range(3)]
+            penalty = fastest * geo8[q, :, 3 * LANES : 4 * LANES]
+            flux = face_flux(outer[k], l2, g2, w2, n)
             for m in range(NQ):
-                sign = sign_s if m < 6 else sign_v
-                flx[q, :, m * LANES : (m + 1) * LANES] = penalty * (u[m] - sign * o[m]) - flux[m]
+                lanes = slice(m * LANES, (m + 1) * LANES)
+                flx[q, :, lanes] = penalty * (own[q, :, lanes] - outer[k][m]) + (base[q, :, lanes] - flux[m])
 
     surface = mm(lift, flx[...].reshape(8 * FQ, WIDE).astype(BF16))
 
-    for dx, dy in ORDER[12:]:
-        chip_products(dx, dy)
+    for i, (dx, dy) in enumerate(LAST):
+        chip_products(dx, dy, i, 16 * len(LAST), fx_b)
 
     all_metric().wait_send()
     all_traces().wait_send()
-    volume = mm(vgm[...], fx[...])
+    volume = acc[...] + mm(vg_b[...], fx_b[...])
     for t in range(2):
         rows = slice(t * BP, (t + 1) * BP)
         lanes = slice(t * LANES, (t + 1) * LANES)
@@ -416,8 +457,13 @@
             pltpu.VMEM((FQ, 8, WIDE), F32),
             pltpu.VMEM((8 * PITCH, LANES), F32),
             pltpu.VMEM((FQ, 8, WIDE), F32),
-            pltpu.VMEM((3 * 256, WIDE), BF16),
-            pltpu.VMEM((2 * BP, 3 * 256), BF16),
+            pltpu.VMEM((48 * len(FIRST), WIDE), BF16),
+            pltpu.VMEM((48 * len(LAST), WIDE), BF16),
+            pltpu.VMEM((2 * BP, 48 * len(FIRST)), BF16),
+            pltpu.VMEM((2 * BP, 48 * len(LAST)), BF16),
+            pltpu.VMEM((2 * BP, WIDE), F32),
+            pltpu.VMEM((FQ, 8, WIDE), F32),
+            pltpu.VMEM((FQ, 8, 4 * LANES), F32),
             dma((len(args),)), pltpu.SemaphoreType.DMA, dma((ROWS,)), pltpu.SemaphoreType.DMA, pltpu.SemaphoreType.DMA,
             pltpu.SemaphoreType.REGULAR,
         ],

time: 18.1 us -> 17.9 us (0.989)
  no operation moved by 1% of the time
where the time goes in v6:
time: 17.9 us; the launch traced here: 17.8 us
  Pallas kernels  17.1 us (96%)
  local copies, waits for them, and re-layouts  0.74 us (4%)
    pallas_call x1, Pallas kernels, per_device(): pl.pallas_call(kernel, out_shape=jax.ShapeDtypeStruct((NQ, NB, E), F32),...  17.1 us
    unnamed x1, local copies, waits for them, and re-layouts  0.74 us

profile of v6, /device:TPU:1, one launch (start us, length us, event | category | flops | bytes accessed | tf_op | source)
XLA Modules:
  0.0 17.8 jit_solution(13802904951780571062)
XLA Ops:
  0.0 17.1 %section.1 = f32[9,35,256]{2,1,0:T(8,128)S(1)} custom-call(f32[9,35,256]{2,1,0:T(8,128)} %state.1, bf16[9,64,4,128]{3,2,1,0:T(4,128)(2,1)} %bitcast.5, f32[4,256]{1,0:T(4,128)} %material.1, s32[4,4,256]{2,1,0:T(4,128)} %neighbours.1, s32[1,8,64]{2,1,0:T(8,128)} %send_faces.1, f32[35,128]{1,0:T(8,128)} %vol_eval.1, bf16[3,35,128]{2,1,0:T(8,128)(2,1)} %vol_grad.1, ...), custom_call_target="tpu_custom_call" | custom-call | tf_op jit(solution)/shard_map/section/pallas_call | solution.py:440
  17.1 0.7 %copy.13 = f32[9,35,256]{2,1,0:T(8,128)} copy(f32[9,35,256]{2,1,0:T(8,128)S(1)} %section.1) | data formatting | bytes 645120

commit v7 on v6

--- a/solution.py
+++ b/solution.py
@@ -19,7 +19,7 @@
 KP = NQ * BP + 8
 PITCH = 264
 ORDER = FAR[-1:] + FAR[:-1]
-FIRST, LAST = ORDER[:12], ORDER[12:]
+FIRST, LAST = ORDER[:8], ORDER[8:]
 
 
 def iota(shape, dim):
@@ -101,11 +101,11 @@
     def signal(sem, r, c):
         pl.semaphore_signal(sem, inc=1, device_id={"row": r, "col": c}, device_id_type=MESH)
 
+    for dx, dy in FAR[:-1]:
+        signal(barrier, 2 * neighbour(dx, dy) + 1, col)
+
     for d in (4, 3, 5, 2, 6, 1, 7):
         signal(barrier, 2 * chip, lax.rem(col + d, COLS))
-
-    for dx, dy in FAR[:-1]:
-        signal(barrier, 2 * neighbour(dx, dy) + 1, col)
 
     signal(barrier, 2 * chip + (1 - core), col)
 
@@ -196,15 +196,17 @@
         def _(i):
             trace_copy(i + jnp.where(i >= col, 1, 0), col).start()
 
-    def send_metric():
-        stage.wait()
+    def send_metric(first, last):
         far = (chip != 0) & (col == 0)
 
-        @pl.when(far)
-        def _():
-            metric_copy(1, row).start()
-
-        for dx, dy in FAR[:-1]:
+        if first == 0:
+            stage.wait()
+
+            @pl.when(far)
+            def _():
+                metric_copy(1, row).start()
+
+        for dx, dy in FAR[first:last]:
             peer = neighbour(dx, dy)
 
             @pl.when(jnp.logical_not(far & (peer == 0)))
@@ -212,21 +214,23 @@
                 metric_copy(2 * peer + 1, row).start()
 
             metric_copy(2 * peer, row).start()
-        metric_copy(2 * chip + (1 - core), row).start()
+        if last == CHIPS - 1:
+            metric_copy(2 * chip + (1 - core), row).start()
 
     @pl.when(col >= EARLY)
     def _():
         wait_column()
         send_traces()
         wait_plane()
-        send_metric()
+        send_metric(0, CHIPS - 1)
 
     @pl.when(col < EARLY)
     def _():
         wait_plane()
-        send_metric()
+        send_metric(0, 8)
         wait_column()
         send_traces()
+        send_metric(8, CHIPS - 1)
 
     for i in (2, 4, 5, 7, 8, 9):
         loads[i].wait()
@@ -350,6 +354,16 @@
         chip_products(dx, dy, i, 16 * len(FIRST), fx_a)
     acc[...] = mm(vg_a[...], fx_a[...])
 
+    def products_of_last(first, last):
+        for i in range(first, last):
+            chip_products(*LAST[i], i, 16 * len(LAST), fx_b)
+
+    traces_late = (col == 1) | (col == 2)
+
+    @pl.when(traces_late)
+    def _():
+        products_of_last(0, 4)
+
     def all_traces():
         part = xr.at[pl.ds(0, COLS - 1)]
         return pltpu.make_async_remote_copy(
@@ -396,8 +410,11 @@
 
     surface = mm(lift, flx[...].reshape(8 * FQ, WIDE).astype(BF16))
 
-    for i, (dx, dy) in enumerate(LAST):
-        chip_products(dx, dy, i, 16 * len(LAST), fx_b)
+    @pl.when(jnp.logical_not(traces_late))
+    def _():
+        products_of_last(0, 4)
+
+    products_of_last(4, len(LAST))
 
     all_metric().wait_send()
     all_traces().wait_send()
@@ -455,7 +472,7 @@
             pltpu.VMEM((256, FACES * E), BF16),
             pltpu.VMEM((256, WIDE), F32),
             pltpu.VMEM((FQ, 8, WIDE), F32),
-            pltpu.VMEM((8 * PITCH, LANES), F32),
+            pltpu.VMEM((9 * PITCH, LANES), F32),
             pltpu.VMEM((FQ, 8, WIDE), F32),
             pltpu.VMEM((48 * len(FIRST), WIDE), BF16),
             pltpu.VMEM((48 * len(LAST), WIDE), BF16),

time: 17.9 us -> 17.6 us (0.983)
  Pallas kernels: 17.1 us -> 16.6 us
    pallas_call x1, Pallas kernels: 17.1 us -> 16.6 us  [per_device(): pl.pallas_call(kernel, out_shape=jax.ShapeDtypeStruct((NQ, NB, E), F32),...]
where the time goes in v7:
time: 17.6 us; the launch traced here: 17.4 us
  Pallas kernels  16.6 us (94%)
  local copies, waits for them, and re-layouts  0.74 us (4%)
    pallas_call x1, Pallas kernels, per_device(): pl.pallas_call(kernel, out_shape=jax.ShapeDtypeStruct((NQ, NB, E), F32),...  16.6 us
    unnamed x1, local copies, waits for them, and re-layouts  0.74 us

profile of v7, /device:TPU:1, one launch (start us, length us, event | category | flops | bytes accessed | tf_op | source)
XLA Modules:
  0.0 17.4 jit_solution(1927155330204533818)
XLA Ops:
  0.0 16.6 %section.1 = f32[9,35,256]{2,1,0:T(8,128)S(1)} custom-call(f32[9,35,256]{2,1,0:T(8,128)} %state.1, bf16[9,64,4,128]{3,2,1,0:T(4,128)(2,1)} %bitcast.5, f32[4,256]{1,0:T(4,128)} %material.1, s32[4,4,256]{2,1,0:T(4,128)} %neighbours.1, s32[1,8,64]{2,1,0:T(8,128)} %send_faces.1, f32[35,128]{1,0:T(8,128)} %vol_eval.1, bf16[3,35,128]{2,1,0:T(8,128)(2,1)} %vol_grad.1, ...), custom_call_target="tpu_custom_call" | custom-call | tf_op jit(solution)/shard_map/section/pallas_call | solution.py:457
  16.6 0.7 %copy.13 = f32[9,35,256]{2,1,0:T(8,128)} copy(f32[9,35,256]{2,1,0:T(8,128)S(1)} %section.1) | data formatting | bytes 645120
